TPU v7x, 256 devices: a whole 4x4x8 slice. The times are simulated.
256 devices in a mesh: col: 32 (over z, y), row: 8 (over x, core).
Axes of the slice: x: 4, y: 4, z: 8, core: 2. Of those that a mesh axis runs over, the one named last changes fastest.
Arguments:
- f_rhs: float32 [256, 1024, 96], P('row', 'col')
- u_init: float32 [256, 1024, 96], P('row', 'col')
- kappa_cell: float32 [256, 1024], P('row', 'col')
- solve_mats: bfloat16 [8, 32, 1024, 2304], P('row', 'col')
- omega_relax: float32 [], replicated
Outputs:
- output: float32 [256, 1024, 96], P('row', 'col')
All inputs are finite; a program needn't handle non-finite values.
Results may differ from a plain program's by a relative error of at most 0.00191557.
Values are sent between devices in bfloat16 or wider.
A program may use at most 768 MiB of HBM per device.

v0:
```python
import math
import jax
import jax.numpy as jnp
from jax import lax
from jax.sharding import PartitionSpec as P

SWEEPS = 6


def shift_from(values, axis_name, axis_size, from_prev):
    if from_prev:
        pair_list = [(i, i + 1) for i in range(axis_size - 1)]
    else:
        pair_list = [(i + 1, i) for i in range(axis_size - 1)]
    return lax.ppermute(values, axis_name, pair_list)


def local_faces(kappa_blk, row_count, col_count):
    from_above = shift_from(kappa_blk[-1:, :], 'row', row_count, True)
    from_below = shift_from(kappa_blk[:1, :], 'row', row_count, False)
    from_left = shift_from(kappa_blk[:, -1:], 'col', col_count, True)
    from_right = shift_from(kappa_blk[:, :1], 'col', col_count, False)
    row_pos = lax.axis_index('row')
    col_pos = lax.axis_index('col')
    inner_v = 0.5 * (kappa_blk[1:, :] + kappa_blk[:-1, :])
    inner_h = 0.5 * (kappa_blk[:, 1:] + kappa_blk[:, :-1])
    edge_n = jnp.where(row_pos == 0, kappa_blk[:1, :], 0.5 * (kappa_blk[:1, :] + from_above))
    edge_s = jnp.where(row_pos == row_count - 1, kappa_blk[-1:, :], 0.5 * (from_below + kappa_blk[-1:, :]))
    edge_w = jnp.where(col_pos == 0, kappa_blk[:, :1], 0.5 * (kappa_blk[:, :1] + from_left))
    edge_e = jnp.where(col_pos == col_count - 1, kappa_blk[:, -1:], 0.5 * (from_right + kappa_blk[:, -1:]))
    face_n = jnp.concatenate([edge_n, inner_v], axis=0)
    face_s = jnp.concatenate([inner_v, edge_s], axis=0)
    face_w = jnp.concatenate([edge_w, inner_h], axis=1)
    face_e = jnp.concatenate([inner_h, edge_e], axis=1)
    return face_n, face_s, face_w, face_e


def apply_local(values, face_set, row_count, col_count):
    face_n, face_s, face_w, face_e = face_set
    from_above = shift_from(values[-1:], 'row', row_count, True).astype(jnp.float32)
    from_below = shift_from(values[:1], 'row', row_count, False).astype(jnp.float32)
    from_left = shift_from(values[:, -1:], 'col', col_count, True).astype(jnp.float32)
    from_right = shift_from(values[:, :1], 'col', col_count, False).astype(jnp.float32)
    center = values.astype(jnp.float32)
    up_nb = jnp.concatenate([from_above, center[:-1]], axis=0)
    down_nb = jnp.concatenate([center[1:], from_below], axis=0)
    left_nb = jnp.concatenate([from_left, center[:, :-1]], axis=1)
    right_nb = jnp.concatenate([center[:, 1:], from_right], axis=1)
    diag_sum = (face_n + face_s + face_w + face_e)[:, :, None]
    return (diag_sum * center
            - face_n[:, :, None] * up_nb
            - face_s[:, :, None] * down_nb
            - face_w[:, :, None] * left_nb
            - face_e[:, :, None] * right_nb)


def extend_block(res_bf, halo_depth, row_count, col_count):
    top_strip = shift_from(res_bf[-halo_depth:], 'row', row_count, True)
    bottom_strip = shift_from(res_bf[:halo_depth], 'row', row_count, False)
    tall_ext = jnp.concatenate([top_strip, res_bf, bottom_strip], axis=0)
    left_strip = shift_from(tall_ext[:, -halo_depth:], 'col', col_count, True)
    right_strip = shift_from(tall_ext[:, :halo_depth], 'col', col_count, False)
    return jnp.concatenate([left_strip, tall_ext, right_strip], axis=1)


def solution(mesh):
    row_count = mesh.shape['row']
    col_count = mesh.shape['col']
    grid_spec = P('row', 'col', None)

    def device_fn(f_blk, u_blk, kappa_blk, mat_blk, omega_relax):
        sub_size = u_blk.shape[0]
        rhs_count = u_blk.shape[2]
        ext_cells = mat_blk.shape[3]
        ext_size = math.isqrt(ext_cells)
        halo_depth = (ext_size - sub_size) // 2
        solve_mat = mat_blk[0, 0]
        face_set = local_faces(kappa_blk, row_count, col_count)
        residual = f_blk - apply_local(u_blk, face_set, row_count, col_count)
        u_cur = u_blk
        for sweep_idx in range(SWEEPS):
            ext_block = extend_block(residual.astype(jnp.bfloat16), halo_depth, row_count, col_count)
            local_z = jnp.dot(solve_mat, ext_block.reshape(ext_cells, rhs_count), preferred_element_type=jnp.float32)
            corr_bf = local_z.astype(jnp.bfloat16).reshape(sub_size, sub_size, rhs_count)
            u_cur = u_cur + omega_relax * corr_bf.astype(jnp.float32)
            if sweep_idx < SWEEPS - 1:
                residual = residual - omega_relax * apply_local(corr_bf, face_set, row_count, col_count)
        return u_cur

    return jax.shard_map(device_fn, mesh=mesh,
                         in_specs=(grid_spec, grid_spec, P('row', 'col'), P('row', 'col', None, None), P()),
                         out_specs=grid_spec, check_vma=False)
```

profile of v0, /device:TPU:121, one launch (start us, length us, event | category | flops | bytes accessed | tf_op | source)
XLA Modules:
  0.0 262.5 jit_solution(5633824196206657676)
XLA Ops:
  0.8 2.6 collective-permute-start.1
  3.3 3.0 %collective-permute-start = (f32[1,32]{1,0:T(1,128)S(1)}, f32[1,32]{1,0:T(1,128)S(1)}, u32[]{:S(2)}, u32[]{:S(2)}) collective-permute-start(f32[1,32]{1,0:T(1,128)S(1)} %get-tuple-element.99), channel_id=1, source_target_pairs={{0,1},{1,2},{2,3},{3,4},{4,5},{5,6},{6,7},{8,9},{9,10},{10,11},{11... | collective-permute-start | bytes 392 | tf_op jit(solution)/shard_map/ppermute | solution.py:15
  7.4 4.4 %collective-permute-start.6 = (f32[32,1,96]{2,1,0:T(1,128)S(1)}, f32[32,1,96]{2,1,0:T(1,128)S(1)}, u32[]{:S(2)}, u32[]{:S(2)}) collective-permute-start(f32[32,1,96]{2,1,0:T(1,128)S(1)} %get-tuple-element.24), channel_id=1, source_target_pairs={{0,8},{8,16},{16,24},{24,32},{32,40},{40,48},{48,56},{56,64},{64,7... | collective-permute-start | bytes 36872 | tf_op jit(solution)/shard_map/ppermute | solution.py:15
  11.8 1.9 collective-permute-start.7
  14.5 2.7 %collective-permute-start.4 = (f32[1,32,96]{2,1,0:T(8,128)S(1)}, f32[1,32,96]{2,1,0:T(8,128)S(1)}, u32[]{:S(2)}, u32[]{:S(2)}) collective-permute-start(f32[1,32,96]{2,1,0:T(8,128)S(1)} %get-tuple-element.20), channel_id=1, source_target_pairs={{0,1},{1,2},{2,3},{3,4},{4,5},{5,6},{6,7},{8,9},{9,10},{10,11},{11... | collective-permute-start | bytes 36872 | tf_op jit(solution)/shard_map/ppermute | solution.py:15
  23.0 7.0 %collective-permute-start.2 = (f32[32,1]{1,0:T(8,128)S(1)}, f32[32,1]{1,0:T(8,128)S(1)}, u32[]{:S(2)}, u32[]{:S(2)}) collective-permute-start(f32[32,1]{1,0:T(8,128)S(1)} %get-tuple-element.95), channel_id=1, source_target_pairs={{0,8},{8,16},{16,24},{24,32},{32,40},{40,48},{48,56},{56,64},{64,7... | collective-permute-start | bytes 392 | tf_op jit(solution)/shard_map/ppermute | solution.py:15
  32.2 2.9 %collective-permute-done.5 = f32[1,32,96]{2,1,0:T(8,128)S(1)} collective-permute-done((f32[1,32,96]{2,1,0:T(8,128)S(1)}, f32[1,32,96]{2,1,0:T(8,128)S(1)}, u32[]{:S(2)}, u32[]{:S(2)}) %collective-permute-start.5) | collective-permute-done | bytes 12320 | tf_op jit(solution)/shard_map/ppermute | solution.py:15
  37.0 1.9 collective-permute-start.8
  38.9 2.4 collective-permute-start.9
  41.3 3.2 %collective-permute-done.9 = bf16[8,32,96]{2,1,0:T(8,128)(2,1)S(1)} collective-permute-done((bf16[8,32,96]{2,1,0:T(8,128)(2,1)S(1)}, bf16[8,32,96]{2,1,0:T(8,128)(2,1)S(1)}, u32[]{:S(2)}, u32[]{:S(2)}) %collective-permute-start.9) | collective-permute-done | bytes 49184 | tf_op jit(solution)/shard_map/ppermute | solution.py:15
  44.5 4.9 %collective-permute-start.10 = (bf16[48,8,96]{2,1,0:T(8,128)(2,1)S(1)}, bf16[48,8,96]{2,1,0:T(8,128)(2,1)S(1)}, u32[]{:S(2)}, u32[]{:S(2)}) collective-permute-start(bf16[48,8,96]{2,1,0:T(8,128)(2,1)S(1)} %get-tuple-element.38), channel_id=1, source_target_pairs={{0,8},{8,16},{16,24},{24,32},{32,40},{40,48},{48,56},{56,64},{64,7... | collective-permute-start | bytes 221192 | tf_op jit(solution)/shard_map/ppermute | solution.py:15
  52.0 6.1 %collective-permute-done.11 = bf16[48,8,96]{2,1,0:T(8,128)(2,1)S(1)} collective-permute-done((bf16[48,8,96]{2,1,0:T(8,128)(2,1)S(1)}, bf16[48,8,96]{2,1,0:T(8,128)(2,1)S(1)}, u32[]{:S(2)}, u32[]{:S(2)}) %collective-permute-start.11) | collective-permute-done | bytes 73760 | tf_op jit(solution)/shard_map/ppermute | solution.py:15
  58.2 3.9 %fusion.24 = bf16[96,1024]{0,1:T(8,128)(2,1)S(1)} fusion(bf16[2304,96]{1,0:T(8,128)(2,1)S(1)} %bitcast.115, bf16[1,1,1024,2304]{3,2,1,0:T(8,128)(2,1)} %param.8), kind=kOutput, calls=%fused_computation.16 | convolution fusion | flops 453083136 | bytes 5357568 | tf_op jit(solution)/shard_map/dot_general | solution.py:83
  62.3 4.1 %collective-permute-start.12 = (bf16[1,32,96]{2,1,0:T(8,128)(2,1)S(1)}, bf16[1,32,96]{2,1,0:T(8,128)(2,1)S(1)}, u32[]{:S(2)}, u32[]{:S(2)}) collective-permute-start(bf16[1,32,96]{2,1,0:T(8,128)(2,1)S(1)} %get-tuple-element.82), channel_id=1, source_target_pairs={{0,1},{1,2},{2,3},{3,4},{4,5},{5,6},{6,7},{8,9},{9,10},{10,11},{11... | collective-permute-start | bytes 18440 | tf_op jit(solution)/shard_map/ppermute | solution.py:15
  70.3 3.4 %collective-permute-start.15 = (bf16[32,1,96]{2,1,0:T(2,128)(2,1)S(1)}, bf16[32,1,96]{2,1,0:T(2,128)(2,1)S(1)}, u32[]{:S(2)}, u32[]{:S(2)}) collective-permute-start(bf16[32,1,96]{2,1,0:T(2,128)(2,1)S(1)} %get-tuple-element.87), channel_id=1, source_target_pairs={{8,0},{16,8},{24,16},{32,24},{40,32},{48,40},{56,48},{64,56},{72,6... | collective-permute-start | bytes 18440 | tf_op jit(solution)/shard_map/ppermute | solution.py:15
  73.9 4.2 %collective-permute-done.15 = bf16[32,1,96]{2,1,0:T(2,128)(2,1)S(1)} collective-permute-done((bf16[32,1,96]{2,1,0:T(2,128)(2,1)S(1)}, bf16[32,1,96]{2,1,0:T(2,128)(2,1)S(1)}, u32[]{:S(2)}, u32[]{:S(2)}) %collective-permute-start.15) | collective-permute-done | bytes 6176 | tf_op jit(solution)/shard_map/ppermute | solution.py:15
  79.1 4.8 %collective-permute-start.16 = (bf16[8,32,96]{2,1,0:T(8,128)(2,1)S(1)}, bf16[8,32,96]{2,1,0:T(8,128)(2,1)S(1)}, u32[]{:S(2)}, u32[]{:S(2)}) collective-permute-start(bf16[8,32,96]{2,1,0:T(8,128)(2,1)S(1)} %get-tuple-element.80), channel_id=1, source_target_pairs={{0,1},{1,2},{2,3},{3,4},{4,5},{5,6},{6,7},{8,9},{9,10},{10,11},{11... | collective-permute-start | bytes 147464 | tf_op jit(solution)/shard_map/ppermute | solution.py:15
  85.8 3.6 %collective-permute-done.17 = bf16[8,32,96]{2,1,0:T(8,128)(2,1)S(1)} collective-permute-done((bf16[8,32,96]{2,1,0:T(8,128)(2,1)S(1)}, bf16[8,32,96]{2,1,0:T(8,128)(2,1)S(1)}, u32[]{:S(2)}, u32[]{:S(2)}) %collective-permute-start.17) | collective-permute-done | bytes 49184 | tf_op jit(solution)/shard_map/ppermute | solution.py:15
  91.4 3.4 %collective-permute-start.19 = (bf16[48,8,96]{2,1,0:T(8,128)(2,1)S(1)}, bf16[48,8,96]{2,1,0:T(8,128)(2,1)S(1)}, u32[]{:S(2)}, u32[]{:S(2)}) collective-permute-start(bf16[48,8,96]{2,1,0:T(8,128)(2,1)S(1)} %get-tuple-element.37), channel_id=1, source_target_pairs={{8,0},{16,8},{24,16},{32,24},{40,32},{48,40},{56,48},{64,56},{72,6... | collective-permute-start | bytes 221192 | tf_op jit(solution)/shard_map/ppermute | solution.py:15
  94.9 5.2 %collective-permute-done.19 = bf16[48,8,96]{2,1,0:T(8,128)(2,1)S(1)} collective-permute-done((bf16[48,8,96]{2,1,0:T(8,128)(2,1)S(1)}, bf16[48,8,96]{2,1,0:T(8,128)(2,1)S(1)}, u32[]{:S(2)}, u32[]{:S(2)}) %collective-permute-start.19) | collective-permute-done | bytes 73760 | tf_op jit(solution)/shard_map/ppermute | solution.py:15
  101.8 3.4 %collective-permute-start.20 = (bf16[1,32,96]{2,1,0:T(8,128)(2,1)S(1)}, bf16[1,32,96]{2,1,0:T(8,128)(2,1)S(1)}, u32[]{:S(2)}, u32[]{:S(2)}) collective-permute-start(bf16[1,32,96]{2,1,0:T(8,128)(2,1)S(1)} %get-tuple-element.72), channel_id=1, source_target_pairs={{0,1},{1,2},{2,3},{3,4},{4,5},{5,6},{6,7},{8,9},{9,10},{10,11},{11... | collective-permute-start | bytes 18440 | tf_op jit(solution)/shard_map/ppermute | solution.py:15
  105.3 1.9 collective-permute-start.21
  109.1 3.4 %collective-permute-start.23 = (bf16[32,1,96]{2,1,0:T(2,128)(2,1)S(1)}, bf16[32,1,96]{2,1,0:T(2,128)(2,1)S(1)}, u32[]{:S(2)}, u32[]{:S(2)}) collective-permute-start(bf16[32,1,96]{2,1,0:T(2,128)(2,1)S(1)} %get-tuple-element.77), channel_id=1, source_target_pairs={{8,0},{16,8},{24,16},{32,24},{40,32},{48,40},{56,48},{64,56},{72,6... | collective-permute-start | bytes 18440 | tf_op jit(solution)/shard_map/ppermute | solution.py:15
  112.7 4.2 %collective-permute-done.23 = bf16[32,1,96]{2,1,0:T(2,128)(2,1)S(1)} collective-permute-done((bf16[32,1,96]{2,1,0:T(2,128)(2,1)S(1)}, bf16[32,1,96]{2,1,0:T(2,128)(2,1)S(1)}, u32[]{:S(2)}, u32[]{:S(2)}) %collective-permute-start.23) | collective-permute-done | bytes 6176 | tf_op jit(solution)/shard_map/ppermute | solution.py:15
  117.9 4.8 %collective-permute-start.24 = (bf16[8,32,96]{2,1,0:T(8,128)(2,1)S(1)}, bf16[8,32,96]{2,1,0:T(8,128)(2,1)S(1)}, u32[]{:S(2)}, u32[]{:S(2)}) collective-permute-start(bf16[8,32,96]{2,1,0:T(8,128)(2,1)S(1)} %get-tuple-element.70), channel_id=1, source_target_pairs={{0,1},{1,2},{2,3},{3,4},{4,5},{5,6},{6,7},{8,9},{9,10},{10,11},{11... | collective-permute-start | bytes 147464 | tf_op jit(solution)/shard_map/ppermute | solution.py:15
  124.6 3.6 %collective-permute-done.25 = bf16[8,32,96]{2,1,0:T(8,128)(2,1)S(1)} collective-permute-done((bf16[8,32,96]{2,1,0:T(8,128)(2,1)S(1)}, bf16[8,32,96]{2,1,0:T(8,128)(2,1)S(1)}, u32[]{:S(2)}, u32[]{:S(2)}) %collective-permute-start.25) | collective-permute-done | bytes 49184 | tf_op jit(solution)/shard_map/ppermute | solution.py:15
  130.2 3.4 %collective-permute-start.27 = (bf16[48,8,96]{2,1,0:T(8,128)(2,1)S(1)}, bf16[48,8,96]{2,1,0:T(8,128)(2,1)S(1)}, u32[]{:S(2)}, u32[]{:S(2)}) collective-permute-start(bf16[48,8,96]{2,1,0:T(8,128)(2,1)S(1)} %get-tuple-element.35), channel_id=1, source_target_pairs={{8,0},{16,8},{24,16},{32,24},{40,32},{48,40},{56,48},{64,56},{72,6... | collective-permute-start | bytes 221192 | tf_op jit(solution)/shard_map/ppermute | solution.py:15
  133.7 5.2 %collective-permute-done.27 = bf16[48,8,96]{2,1,0:T(8,128)(2,1)S(1)} collective-permute-done((bf16[48,8,96]{2,1,0:T(8,128)(2,1)S(1)}, bf16[48,8,96]{2,1,0:T(8,128)(2,1)S(1)}, u32[]{:S(2)}, u32[]{:S(2)}) %collective-permute-start.27) | collective-permute-done | bytes 73760 | tf_op jit(solution)/shard_map/ppermute | solution.py:15
  140.6 3.8 %collective-permute-start.28 = (bf16[1,32,96]{2,1,0:T(8,128)(2,1)S(1)}, bf16[1,32,96]{2,1,0:T(8,128)(2,1)S(1)}, u32[]{:S(2)}, u32[]{:S(2)}) collective-permute-start(bf16[1,32,96]{2,1,0:T(8,128)(2,1)S(1)} %get-tuple-element.62), channel_id=1, source_target_pairs={{0,1},{1,2},{2,3},{3,4},{4,5},{5,6},{6,7},{8,9},{9,10},{10,11},{11... | collective-permute-start | bytes 18440 | tf_op jit(solution)/shard_map/ppermute | solution.py:15
  148.3 3.4 %collective-permute-start.31 = (bf16[32,1,96]{2,1,0:T(2,128)(2,1)S(1)}, bf16[32,1,96]{2,1,0:T(2,128)(2,1)S(1)}, u32[]{:S(2)}, u32[]{:S(2)}) collective-permute-start(bf16[32,1,96]{2,1,0:T(2,128)(2,1)S(1)} %get-tuple-element.67), channel_id=1, source_target_pairs={{8,0},{16,8},{24,16},{32,24},{40,32},{48,40},{56,48},{64,56},{72,6... | collective-permute-start | bytes 18440 | tf_op jit(solution)/shard_map/ppermute | solution.py:15
  151.8 4.3 %collective-permute-done.31 = bf16[32,1,96]{2,1,0:T(2,128)(2,1)S(1)} collective-permute-done((bf16[32,1,96]{2,1,0:T(2,128)(2,1)S(1)}, bf16[32,1,96]{2,1,0:T(2,128)(2,1)S(1)}, u32[]{:S(2)}, u32[]{:S(2)}) %collective-permute-start.31) | collective-permute-done | bytes 6176 | tf_op jit(solution)/shard_map/ppermute | solution.py:15
  157.1 4.8 %collective-permute-start.32 = (bf16[8,32,96]{2,1,0:T(8,128)(2,1)S(1)}, bf16[8,32,96]{2,1,0:T(8,128)(2,1)S(1)}, u32[]{:S(2)}, u32[]{:S(2)}) collective-permute-start(bf16[8,32,96]{2,1,0:T(8,128)(2,1)S(1)} %get-tuple-element.60), channel_id=1, source_target_pairs={{0,1},{1,2},{2,3},{3,4},{4,5},{5,6},{6,7},{8,9},{9,10},{10,11},{11... | collective-permute-start | bytes 147464 | tf_op jit(solution)/shard_map/ppermute | solution.py:15
  163.8 3.6 %collective-permute-done.33 = bf16[8,32,96]{2,1,0:T(8,128)(2,1)S(1)} collective-permute-done((bf16[8,32,96]{2,1,0:T(8,128)(2,1)S(1)}, bf16[8,32,96]{2,1,0:T(8,128)(2,1)S(1)}, u32[]{:S(2)}, u32[]{:S(2)}) %collective-permute-start.33) | collective-permute-done | bytes 49184 | tf_op jit(solution)/shard_map/ppermute | solution.py:15
  169.4 3.4 %collective-permute-start.35 = (bf16[48,8,96]{2,1,0:T(8,128)(2,1)S(1)}, bf16[48,8,96]{2,1,0:T(8,128)(2,1)S(1)}, u32[]{:S(2)}, u32[]{:S(2)}) collective-permute-start(bf16[48,8,96]{2,1,0:T(8,128)(2,1)S(1)} %get-tuple-element.33), channel_id=1, source_target_pairs={{8,0},{16,8},{24,16},{32,24},{40,32},{48,40},{56,48},{64,56},{72,6... | collective-permute-start | bytes 221192 | tf_op jit(solution)/shard_map/ppermute | solution.py:15
  172.8 5.2 %collective-permute-done.35 = bf16[48,8,96]{2,1,0:T(8,128)(2,1)S(1)} collective-permute-done((bf16[48,8,96]{2,1,0:T(8,128)(2,1)S(1)}, bf16[48,8,96]{2,1,0:T(8,128)(2,1)S(1)}, u32[]{:S(2)}, u32[]{:S(2)}) %collective-permute-start.35) | collective-permute-done | bytes 73760 | tf_op jit(solution)/shard_map/ppermute | solution.py:15
  179.8 3.8 %collective-permute-start.36 = (bf16[1,32,96]{2,1,0:T(8,128)(2,1)S(1)}, bf16[1,32,96]{2,1,0:T(8,128)(2,1)S(1)}, u32[]{:S(2)}, u32[]{:S(2)}) collective-permute-start(bf16[1,32,96]{2,1,0:T(8,128)(2,1)S(1)} %get-tuple-element.52), channel_id=1, source_target_pairs={{0,1},{1,2},{2,3},{3,4},{4,5},{5,6},{6,7},{8,9},{9,10},{10,11},{11... | collective-permute-start | bytes 18440 | tf_op jit(solution)/shard_map/ppermute | solution.py:15
  187.4 3.4 %collective-permute-start.39 = (bf16[32,1,96]{2,1,0:T(2,128)(2,1)S(1)}, bf16[32,1,96]{2,1,0:T(2,128)(2,1)S(1)}, u32[]{:S(2)}, u32[]{:S(2)}) collective-permute-start(bf16[32,1,96]{2,1,0:T(2,128)(2,1)S(1)} %get-tuple-element.57), channel_id=1, source_target_pairs={{8,0},{16,8},{24,16},{32,24},{40,32},{48,40},{56,48},{64,56},{72,6... | collective-permute-start | bytes 18440 | tf_op jit(solution)/shard_map/ppermute | solution.py:15
  191.0 4.3 %collective-permute-done.39 = bf16[32,1,96]{2,1,0:T(2,128)(2,1)S(1)} collective-permute-done((bf16[32,1,96]{2,1,0:T(2,128)(2,1)S(1)}, bf16[32,1,96]{2,1,0:T(2,128)(2,1)S(1)}, u32[]{:S(2)}, u32[]{:S(2)}) %collective-permute-start.39) | collective-permute-done | bytes 6176 | tf_op jit(solution)/shard_map/ppermute | solution.py:15
  196.2 4.8 %collective-permute-start.40 = (bf16[8,32,96]{2,1,0:T(8,128)(2,1)S(1)}, bf16[8,32,96]{2,1,0:T(8,128)(2,1)S(1)}, u32[]{:S(2)}, u32[]{:S(2)}) collective-permute-start(bf16[8,32,96]{2,1,0:T(8,128)(2,1)S(1)} %get-tuple-element.50), channel_id=1, source_target_pairs={{0,1},{1,2},{2,3},{3,4},{4,5},{5,6},{6,7},{8,9},{9,10},{10,11},{11... | collective-permute-start | bytes 147464 | tf_op jit(solution)/shard_map/ppermute | solution.py:15
  202.9 3.6 %collective-permute-done.41 = bf16[8,32,96]{2,1,0:T(8,128)(2,1)S(1)} collective-permute-done((bf16[8,32,96]{2,1,0:T(8,128)(2,1)S(1)}, bf16[8,32,96]{2,1,0:T(8,128)(2,1)S(1)}, u32[]{:S(2)}, u32[]{:S(2)}) %collective-permute-start.41) | collective-permute-done | bytes 49184 | tf_op jit(solution)/shard_map/ppermute | solution.py:15
  208.6 3.5 %collective-permute-start.43 = (bf16[48,8,96]{2,1,0:T(8,128)(2,1)S(1)}, bf16[48,8,96]{2,1,0:T(8,128)(2,1)S(1)}, u32[]{:S(2)}, u32[]{:S(2)}) collective-permute-start(bf16[48,8,96]{2,1,0:T(8,128)(2,1)S(1)} %get-tuple-element.31), channel_id=1, source_target_pairs={{8,0},{16,8},{24,16},{32,24},{40,32},{48,40},{56,48},{64,56},{72,6... | collective-permute-start | bytes 221192 | tf_op jit(solution)/shard_map/ppermute | solution.py:15
  212.1 5.1 %collective-permute-done.43 = bf16[48,8,96]{2,1,0:T(8,128)(2,1)S(1)} collective-permute-done((bf16[48,8,96]{2,1,0:T(8,128)(2,1)S(1)}, bf16[48,8,96]{2,1,0:T(8,128)(2,1)S(1)}, u32[]{:S(2)}, u32[]{:S(2)}) %collective-permute-start.43) | collective-permute-done | bytes 73760 | tf_op jit(solution)/shard_map/ppermute | solution.py:15
  220.8 3.6 %collective-permute-start.44 = (bf16[1,32,96]{2,1,0:T(8,128)(2,1)S(1)}, bf16[1,32,96]{2,1,0:T(8,128)(2,1)S(1)}, u32[]{:S(2)}, u32[]{:S(2)}) collective-permute-start(bf16[1,32,96]{2,1,0:T(8,128)(2,1)S(1)} %get-tuple-element.49), channel_id=1, source_target_pairs={{0,1},{1,2},{2,3},{3,4},{4,5},{5,6},{6,7},{8,9},{9,10},{10,11},{11... | collective-permute-start | bytes 18440 | tf_op jit(solution)/shard_map/ppermute | solution.py:15
  226.4 6.7 %collective-permute-start.46 = (bf16[32,1,96]{2,1,0:T(2,128)(2,1)S(1)}, bf16[32,1,96]{2,1,0:T(2,128)(2,1)S(1)}, u32[]{:S(2)}, u32[]{:S(2)}) collective-permute-start(bf16[32,1,96]{2,1,0:T(2,128)(2,1)S(1)} %get-tuple-element.45), channel_id=1, source_target_pairs={{0,8},{8,16},{16,24},{24,32},{32,40},{40,48},{48,56},{56,64},{64,7... | collective-permute-start | bytes 18440 | tf_op jit(solution)/shard_map/ppermute | solution.py:15
  234.9 3.1 %collective-permute-start.48 = (bf16[8,32,96]{2,1,0:T(8,128)(2,1)S(1)}, bf16[8,32,96]{2,1,0:T(8,128)(2,1)S(1)}, u32[]{:S(2)}, u32[]{:S(2)}) collective-permute-start(bf16[8,32,96]{2,1,0:T(8,128)(2,1)S(1)} %get-tuple-element.40), channel_id=1, source_target_pairs={{0,1},{1,2},{2,3},{3,4},{4,5},{5,6},{6,7},{8,9},{9,10},{10,11},{11... | collective-permute-start | bytes 147464 | tf_op jit(solution)/shard_map/ppermute | solution.py:15
  239.9 3.6 %collective-permute-done.49 = bf16[8,32,96]{2,1,0:T(8,128)(2,1)S(1)} collective-permute-done((bf16[8,32,96]{2,1,0:T(8,128)(2,1)S(1)}, bf16[8,32,96]{2,1,0:T(8,128)(2,1)S(1)}, u32[]{:S(2)}, u32[]{:S(2)}) %collective-permute-start.49) | collective-permute-done | bytes 49184 | tf_op jit(solution)/shard_map/ppermute | solution.py:15
  243.6 7.2 %collective-permute-start.50 = (bf16[48,8,96]{2,1,0:T(8,128)(2,1)S(1)}, bf16[48,8,96]{2,1,0:T(8,128)(2,1)S(1)}, u32[]{:S(2)}, u32[]{:S(2)}) collective-permute-start(bf16[48,8,96]{2,1,0:T(8,128)(2,1)S(1)} %get-tuple-element.28), channel_id=1, source_target_pairs={{0,8},{8,16},{16,24},{24,32},{32,40},{40,48},{48,56},{56,64},{64,7... | collective-permute-start | bytes 221192 | tf_op jit(solution)/shard_map/ppermute | solution.py:15
  252.8 6.7 %collective-permute-done.51 = bf16[48,8,96]{2,1,0:T(8,128)(2,1)S(1)} collective-permute-done((bf16[48,8,96]{2,1,0:T(8,128)(2,1)S(1)}, bf16[48,8,96]{2,1,0:T(8,128)(2,1)S(1)}, u32[]{:S(2)}, u32[]{:S(2)}) %collective-permute-start.51) | collective-permute-done | bytes 73760 | tf_op jit(solution)/shard_map/ppermute | solution.py:15
  (148 shorter events, 67.0 us)
Async XLA Ops:
  0.8 20.3 %collective-permute-start.1 = (f32[1,32]{1,0:T(1,128)S(1)}, f32[1,32]{1,0:T(1,128)S(1)}, u32[]{:S(2)}, u32[]{:S(2)}) collective-permute-start(f32[1,32]{1,0:T(1,128)S(1)} %get-tuple-element.98), channel_id=1, source_target_pairs={{1,0},{2,1},{3,2},{4,3},{5,4},{6,5},{7,6},{9,8},{10,9},{11,10},{12... | collective-permute-start | bytes 392 | tf_op jit(solution)/shard_map/ppermute | solution.py:15
  3.3 19.7 %collective-permute-start = (f32[1,32]{1,0:T(1,128)S(1)}, f32[1,32]{1,0:T(1,128)S(1)}, u32[]{:S(2)}, u32[]{:S(2)}) collective-permute-start(f32[1,32]{1,0:T(1,128)S(1)} %get-tuple-element.99), channel_id=1, source_target_pairs={{0,1},{1,2},{2,3},{3,4},{4,5},{5,6},{6,7},{8,9},{9,10},{10,11},{11... | collective-permute-start | bytes 392 | tf_op jit(solution)/shard_map/ppermute | solution.py:15
  7.4 24.8 %collective-permute-start.6 = (f32[32,1,96]{2,1,0:T(1,128)S(1)}, f32[32,1,96]{2,1,0:T(1,128)S(1)}, u32[]{:S(2)}, u32[]{:S(2)}) collective-permute-start(f32[32,1,96]{2,1,0:T(1,128)S(1)} %get-tuple-element.24), channel_id=1, source_target_pairs={{0,8},{8,16},{16,24},{24,32},{32,40},{40,48},{48,56},{56,64},{64,7... | collective-permute-start | bytes 36872 | tf_op jit(solution)/shard_map/ppermute | solution.py:15
  11.8 20.4 %collective-permute-start.7 = (f32[32,1,96]{2,1,0:T(1,128)S(1)}, f32[32,1,96]{2,1,0:T(1,128)S(1)}, u32[]{:S(2)}, u32[]{:S(2)}) collective-permute-start(f32[32,1,96]{2,1,0:T(1,128)S(1)} %get-tuple-element.25), channel_id=1, source_target_pairs={{8,0},{16,8},{24,16},{32,24},{40,32},{48,40},{56,48},{64,56},{72,6... | collective-permute-start | bytes 36872 | tf_op jit(solution)/shard_map/ppermute | solution.py:15
  14.5 17.7 %collective-permute-start.4 = (f32[1,32,96]{2,1,0:T(8,128)S(1)}, f32[1,32,96]{2,1,0:T(8,128)S(1)}, u32[]{:S(2)}, u32[]{:S(2)}) collective-permute-start(f32[1,32,96]{2,1,0:T(8,128)S(1)} %get-tuple-element.20), channel_id=1, source_target_pairs={{0,1},{1,2},{2,3},{3,4},{4,5},{5,6},{6,7},{8,9},{9,10},{10,11},{11... | collective-permute-start | bytes 36872 | tf_op jit(solution)/shard_map/ppermute | solution.py:15
  21.1 8.9 %collective-permute-start.3 = (f32[32,1]{1,0:T(8,128)S(1)}, f32[32,1]{1,0:T(8,128)S(1)}, u32[]{:S(2)}, u32[]{:S(2)}) collective-permute-start(f32[32,1]{1,0:T(8,128)S(1)} %get-tuple-element.94), channel_id=1, source_target_pairs={{8,0},{16,8},{24,16},{32,24},{40,32},{48,40},{56,48},{64,56},{72,6... | collective-permute-start | bytes 392 | tf_op jit(solution)/shard_map/ppermute | solution.py:15
  23.0 8.9 %collective-permute-start.2 = (f32[32,1]{1,0:T(8,128)S(1)}, f32[32,1]{1,0:T(8,128)S(1)}, u32[]{:S(2)}, u32[]{:S(2)}) collective-permute-start(f32[32,1]{1,0:T(8,128)S(1)} %get-tuple-element.95), channel_id=1, source_target_pairs={{0,8},{8,16},{16,24},{24,32},{32,40},{40,48},{48,56},{56,64},{64,7... | collective-permute-start | bytes 392 | tf_op jit(solution)/shard_map/ppermute | solution.py:15
  38.9 5.6 %collective-permute-start.9 = (bf16[8,32,96]{2,1,0:T(8,128)(2,1)S(1)}, bf16[8,32,96]{2,1,0:T(8,128)(2,1)S(1)}, u32[]{:S(2)}, u32[]{:S(2)}) collective-permute-start(bf16[8,32,96]{2,1,0:T(8,128)(2,1)S(1)} %get-tuple-element.91), channel_id=1, source_target_pairs={{1,0},{2,1},{3,2},{4,3},{5,4},{6,5},{7,6},{9,8},{10,9},{11,10},{12... | collective-permute-start | bytes 147464 | tf_op jit(solution)/shard_map/ppermute | solution.py:15
  44.5 7.5 %collective-permute-start.10 = (bf16[48,8,96]{2,1,0:T(8,128)(2,1)S(1)}, bf16[48,8,96]{2,1,0:T(8,128)(2,1)S(1)}, u32[]{:S(2)}, u32[]{:S(2)}) collective-permute-start(bf16[48,8,96]{2,1,0:T(8,128)(2,1)S(1)} %get-tuple-element.38), channel_id=1, source_target_pairs={{0,8},{8,16},{16,24},{24,32},{32,40},{40,48},{48,56},{56,64},{64,7... | collective-permute-start | bytes 221192 | tf_op jit(solution)/shard_map/ppermute | solution.py:15
  49.4 8.7 %collective-permute-start.11 = (bf16[48,8,96]{2,1,0:T(8,128)(2,1)S(1)}, bf16[48,8,96]{2,1,0:T(8,128)(2,1)S(1)}, u32[]{:S(2)}, u32[]{:S(2)}) collective-permute-start(bf16[48,8,96]{2,1,0:T(8,128)(2,1)S(1)} %get-tuple-element.39), channel_id=1, source_target_pairs={{8,0},{16,8},{24,16},{32,24},{40,32},{48,40},{56,48},{64,56},{72,6... | collective-permute-start | bytes 221192 | tf_op jit(solution)/shard_map/ppermute | solution.py:15
  62.3 11.5 %collective-permute-start.12 = (bf16[1,32,96]{2,1,0:T(8,128)(2,1)S(1)}, bf16[1,32,96]{2,1,0:T(8,128)(2,1)S(1)}, u32[]{:S(2)}, u32[]{:S(2)}) collective-permute-start(bf16[1,32,96]{2,1,0:T(8,128)(2,1)S(1)} %get-tuple-element.82), channel_id=1, source_target_pairs={{0,1},{1,2},{2,3},{3,4},{4,5},{5,6},{6,7},{8,9},{9,10},{10,11},{11... | collective-permute-start | bytes 18440 | tf_op jit(solution)/shard_map/ppermute | solution.py:15
  66.4 7.4 %collective-permute-start.13 = (bf16[1,32,96]{2,1,0:T(8,128)(2,1)S(1)}, bf16[1,32,96]{2,1,0:T(8,128)(2,1)S(1)}, u32[]{:S(2)}, u32[]{:S(2)}) collective-permute-start(bf16[1,32,96]{2,1,0:T(8,128)(2,1)S(1)} %get-tuple-element.83), channel_id=1, source_target_pairs={{1,0},{2,1},{3,2},{4,3},{5,4},{6,5},{7,6},{9,8},{10,9},{11,10},{12... | collective-permute-start | bytes 18440 | tf_op jit(solution)/shard_map/ppermute | solution.py:15
  68.4 5.5 %collective-permute-start.14 = (bf16[32,1,96]{2,1,0:T(2,128)(2,1)S(1)}, bf16[32,1,96]{2,1,0:T(2,128)(2,1)S(1)}, u32[]{:S(2)}, u32[]{:S(2)}) collective-permute-start(bf16[32,1,96]{2,1,0:T(2,128)(2,1)S(1)} %get-tuple-element.86), channel_id=1, source_target_pairs={{0,8},{8,16},{16,24},{24,32},{32,40},{40,48},{48,56},{56,64},{64,7... | collective-permute-start | bytes 18440 | tf_op jit(solution)/shard_map/ppermute | solution.py:15
  70.3 7.8 %collective-permute-start.15 = (bf16[32,1,96]{2,1,0:T(2,128)(2,1)S(1)}, bf16[32,1,96]{2,1,0:T(2,128)(2,1)S(1)}, u32[]{:S(2)}, u32[]{:S(2)}) collective-permute-start(bf16[32,1,96]{2,1,0:T(2,128)(2,1)S(1)} %get-tuple-element.87), channel_id=1, source_target_pairs={{8,0},{16,8},{24,16},{32,24},{40,32},{48,40},{56,48},{64,56},{72,6... | collective-permute-start | bytes 18440 | tf_op jit(solution)/shard_map/ppermute | solution.py:15
  79.1 6.7 %collective-permute-start.16 = (bf16[8,32,96]{2,1,0:T(8,128)(2,1)S(1)}, bf16[8,32,96]{2,1,0:T(8,128)(2,1)S(1)}, u32[]{:S(2)}, u32[]{:S(2)}) collective-permute-start(bf16[8,32,96]{2,1,0:T(8,128)(2,1)S(1)} %get-tuple-element.80), channel_id=1, source_target_pairs={{0,1},{1,2},{2,3},{3,4},{4,5},{5,6},{6,7},{8,9},{9,10},{10,11},{11... | collective-permute-start | bytes 147464 | tf_op jit(solution)/shard_map/ppermute | solution.py:15
  83.9 5.6 %collective-permute-start.17 = (bf16[8,32,96]{2,1,0:T(8,128)(2,1)S(1)}, bf16[8,32,96]{2,1,0:T(8,128)(2,1)S(1)}, u32[]{:S(2)}, u32[]{:S(2)}) collective-permute-start(bf16[8,32,96]{2,1,0:T(8,128)(2,1)S(1)} %get-tuple-element.81), channel_id=1, source_target_pairs={{1,0},{2,1},{3,2},{4,3},{5,4},{6,5},{7,6},{9,8},{10,9},{11,10},{12... | collective-permute-start | bytes 147464 | tf_op jit(solution)/shard_map/ppermute | solution.py:15
  89.5 5.4 %collective-permute-start.18 = (bf16[48,8,96]{2,1,0:T(8,128)(2,1)S(1)}, bf16[48,8,96]{2,1,0:T(8,128)(2,1)S(1)}, u32[]{:S(2)}, u32[]{:S(2)}) collective-permute-start(bf16[48,8,96]{2,1,0:T(8,128)(2,1)S(1)} %get-tuple-element.36), channel_id=1, source_target_pairs={{0,8},{8,16},{16,24},{24,32},{32,40},{40,48},{48,56},{56,64},{64,7... | collective-permute-start | bytes 221192 | tf_op jit(solution)/shard_map/ppermute | solution.py:15
  91.4 8.7 %collective-permute-start.19 = (bf16[48,8,96]{2,1,0:T(8,128)(2,1)S(1)}, bf16[48,8,96]{2,1,0:T(8,128)(2,1)S(1)}, u32[]{:S(2)}, u32[]{:S(2)}) collective-permute-start(bf16[48,8,96]{2,1,0:T(8,128)(2,1)S(1)} %get-tuple-element.37), channel_id=1, source_target_pairs={{8,0},{16,8},{24,16},{32,24},{40,32},{48,40},{56,48},{64,56},{72,6... | collective-permute-start | bytes 221192 | tf_op jit(solution)/shard_map/ppermute | solution.py:15
  101.8 10.8 %collective-permute-start.20 = (bf16[1,32,96]{2,1,0:T(8,128)(2,1)S(1)}, bf16[1,32,96]{2,1,0:T(8,128)(2,1)S(1)}, u32[]{:S(2)}, u32[]{:S(2)}) collective-permute-start(bf16[1,32,96]{2,1,0:T(8,128)(2,1)S(1)} %get-tuple-element.72), channel_id=1, source_target_pairs={{0,1},{1,2},{2,3},{3,4},{4,5},{5,6},{6,7},{8,9},{9,10},{10,11},{11... | collective-permute-start | bytes 18440 | tf_op jit(solution)/shard_map/ppermute | solution.py:15
  105.3 7.4 %collective-permute-start.21 = (bf16[1,32,96]{2,1,0:T(8,128)(2,1)S(1)}, bf16[1,32,96]{2,1,0:T(8,128)(2,1)S(1)}, u32[]{:S(2)}, u32[]{:S(2)}) collective-permute-start(bf16[1,32,96]{2,1,0:T(8,128)(2,1)S(1)} %get-tuple-element.73), channel_id=1, source_target_pairs={{1,0},{2,1},{3,2},{4,3},{5,4},{6,5},{7,6},{9,8},{10,9},{11,10},{12... | collective-permute-start | bytes 18440 | tf_op jit(solution)/shard_map/ppermute | solution.py:15
  107.2 5.5 %collective-permute-start.22 = (bf16[32,1,96]{2,1,0:T(2,128)(2,1)S(1)}, bf16[32,1,96]{2,1,0:T(2,128)(2,1)S(1)}, u32[]{:S(2)}, u32[]{:S(2)}) collective-permute-start(bf16[32,1,96]{2,1,0:T(2,128)(2,1)S(1)} %get-tuple-element.76), channel_id=1, source_target_pairs={{0,8},{8,16},{16,24},{24,32},{32,40},{40,48},{48,56},{56,64},{64,7... | collective-permute-start | bytes 18440 | tf_op jit(solution)/shard_map/ppermute | solution.py:15
  109.1 7.8 %collective-permute-start.23 = (bf16[32,1,96]{2,1,0:T(2,128)(2,1)S(1)}, bf16[32,1,96]{2,1,0:T(2,128)(2,1)S(1)}, u32[]{:S(2)}, u32[]{:S(2)}) collective-permute-start(bf16[32,1,96]{2,1,0:T(2,128)(2,1)S(1)} %get-tuple-element.77), channel_id=1, source_target_pairs={{8,0},{16,8},{24,16},{32,24},{40,32},{48,40},{56,48},{64,56},{72,6... | collective-permute-start | bytes 18440 | tf_op jit(solution)/shard_map/ppermute | solution.py:15
  117.9 6.7 %collective-permute-start.24 = (bf16[8,32,96]{2,1,0:T(8,128)(2,1)S(1)}, bf16[8,32,96]{2,1,0:T(8,128)(2,1)S(1)}, u32[]{:S(2)}, u32[]{:S(2)}) collective-permute-start(bf16[8,32,96]{2,1,0:T(8,128)(2,1)S(1)} %get-tuple-element.70), channel_id=1, source_target_pairs={{0,1},{1,2},{2,3},{3,4},{4,5},{5,6},{6,7},{8,9},{9,10},{10,11},{11... | collective-permute-start | bytes 147464 | tf_op jit(solution)/shard_map/ppermute | solution.py:15
  122.7 5.6 %collective-permute-start.25 = (bf16[8,32,96]{2,1,0:T(8,128)(2,1)S(1)}, bf16[8,32,96]{2,1,0:T(8,128)(2,1)S(1)}, u32[]{:S(2)}, u32[]{:S(2)}) collective-permute-start(bf16[8,32,96]{2,1,0:T(8,128)(2,1)S(1)} %get-tuple-element.71), channel_id=1, source_target_pairs={{1,0},{2,1},{3,2},{4,3},{5,4},{6,5},{7,6},{9,8},{10,9},{11,10},{12... | collective-permute-start | bytes 147464 | tf_op jit(solution)/shard_map/ppermute | solution.py:15
  128.3 5.4 %collective-permute-start.26 = (bf16[48,8,96]{2,1,0:T(8,128)(2,1)S(1)}, bf16[48,8,96]{2,1,0:T(8,128)(2,1)S(1)}, u32[]{:S(2)}, u32[]{:S(2)}) collective-permute-start(bf16[48,8,96]{2,1,0:T(8,128)(2,1)S(1)} %get-tuple-element.34), channel_id=1, source_target_pairs={{0,8},{8,16},{16,24},{24,32},{32,40},{40,48},{48,56},{56,64},{64,7... | collective-permute-start | bytes 221192 | tf_op jit(solution)/shard_map/ppermute | solution.py:15
  130.2 8.7 %collective-permute-start.27 = (bf16[48,8,96]{2,1,0:T(8,128)(2,1)S(1)}, bf16[48,8,96]{2,1,0:T(8,128)(2,1)S(1)}, u32[]{:S(2)}, u32[]{:S(2)}) collective-permute-start(bf16[48,8,96]{2,1,0:T(8,128)(2,1)S(1)} %get-tuple-element.35), channel_id=1, source_target_pairs={{8,0},{16,8},{24,16},{32,24},{40,32},{48,40},{56,48},{64,56},{72,6... | collective-permute-start | bytes 221192 | tf_op jit(solution)/shard_map/ppermute | solution.py:15
  140.6 11.1 %collective-permute-start.28 = (bf16[1,32,96]{2,1,0:T(8,128)(2,1)S(1)}, bf16[1,32,96]{2,1,0:T(8,128)(2,1)S(1)}, u32[]{:S(2)}, u32[]{:S(2)}) collective-permute-start(bf16[1,32,96]{2,1,0:T(8,128)(2,1)S(1)} %get-tuple-element.62), channel_id=1, source_target_pairs={{0,1},{1,2},{2,3},{3,4},{4,5},{5,6},{6,7},{8,9},{9,10},{10,11},{11... | collective-permute-start | bytes 18440 | tf_op jit(solution)/shard_map/ppermute | solution.py:15
  144.4 7.3 %collective-permute-start.29 = (bf16[1,32,96]{2,1,0:T(8,128)(2,1)S(1)}, bf16[1,32,96]{2,1,0:T(8,128)(2,1)S(1)}, u32[]{:S(2)}, u32[]{:S(2)}) collective-permute-start(bf16[1,32,96]{2,1,0:T(8,128)(2,1)S(1)} %get-tuple-element.63), channel_id=1, source_target_pairs={{1,0},{2,1},{3,2},{4,3},{5,4},{6,5},{7,6},{9,8},{10,9},{11,10},{12... | collective-permute-start | bytes 18440 | tf_op jit(solution)/shard_map/ppermute | solution.py:15
  146.4 5.4 %collective-permute-start.30 = (bf16[32,1,96]{2,1,0:T(2,128)(2,1)S(1)}, bf16[32,1,96]{2,1,0:T(2,128)(2,1)S(1)}, u32[]{:S(2)}, u32[]{:S(2)}) collective-permute-start(bf16[32,1,96]{2,1,0:T(2,128)(2,1)S(1)} %get-tuple-element.66), channel_id=1, source_target_pairs={{0,8},{8,16},{16,24},{24,32},{32,40},{40,48},{48,56},{56,64},{64,7... | collective-permute-start | bytes 18440 | tf_op jit(solution)/shard_map/ppermute | solution.py:15
  148.3 7.8 %collective-permute-start.31 = (bf16[32,1,96]{2,1,0:T(2,128)(2,1)S(1)}, bf16[32,1,96]{2,1,0:T(2,128)(2,1)S(1)}, u32[]{:S(2)}, u32[]{:S(2)}) collective-permute-start(bf16[32,1,96]{2,1,0:T(2,128)(2,1)S(1)} %get-tuple-element.67), channel_id=1, source_target_pairs={{8,0},{16,8},{24,16},{32,24},{40,32},{48,40},{56,48},{64,56},{72,6... | collective-permute-start | bytes 18440 | tf_op jit(solution)/shard_map/ppermute | solution.py:15
  157.1 6.7 %collective-permute-start.32 = (bf16[8,32,96]{2,1,0:T(8,128)(2,1)S(1)}, bf16[8,32,96]{2,1,0:T(8,128)(2,1)S(1)}, u32[]{:S(2)}, u32[]{:S(2)}) collective-permute-start(bf16[8,32,96]{2,1,0:T(8,128)(2,1)S(1)} %get-tuple-element.60), channel_id=1, source_target_pairs={{0,1},{1,2},{2,3},{3,4},{4,5},{5,6},{6,7},{8,9},{9,10},{10,11},{11... | collective-permute-start | bytes 147464 | tf_op jit(solution)/shard_map/ppermute | solution.py:15
  161.9 5.6 %collective-permute-start.33 = (bf16[8,32,96]{2,1,0:T(8,128)(2,1)S(1)}, bf16[8,32,96]{2,1,0:T(8,128)(2,1)S(1)}, u32[]{:S(2)}, u32[]{:S(2)}) collective-permute-start(bf16[8,32,96]{2,1,0:T(8,128)(2,1)S(1)} %get-tuple-element.61), channel_id=1, source_target_pairs={{1,0},{2,1},{3,2},{4,3},{5,4},{6,5},{7,6},{9,8},{10,9},{11,10},{12... | collective-permute-start | bytes 147464 | tf_op jit(solution)/shard_map/ppermute | solution.py:15
  169.4 8.7 %collective-permute-start.35 = (bf16[48,8,96]{2,1,0:T(8,128)(2,1)S(1)}, bf16[48,8,96]{2,1,0:T(8,128)(2,1)S(1)}, u32[]{:S(2)}, u32[]{:S(2)}) collective-permute-start(bf16[48,8,96]{2,1,0:T(8,128)(2,1)S(1)} %get-tuple-element.33), channel_id=1, source_target_pairs={{8,0},{16,8},{24,16},{32,24},{40,32},{48,40},{56,48},{64,56},{72,6... | collective-permute-start | bytes 221192 | tf_op jit(solution)/shard_map/ppermute | solution.py:15
  179.8 11.1 %collective-permute-start.36 = (bf16[1,32,96]{2,1,0:T(8,128)(2,1)S(1)}, bf16[1,32,96]{2,1,0:T(8,128)(2,1)S(1)}, u32[]{:S(2)}, u32[]{:S(2)}) collective-permute-start(bf16[1,32,96]{2,1,0:T(8,128)(2,1)S(1)} %get-tuple-element.52), channel_id=1, source_target_pairs={{0,1},{1,2},{2,3},{3,4},{4,5},{5,6},{6,7},{8,9},{9,10},{10,11},{11... | collective-permute-start | bytes 18440 | tf_op jit(solution)/shard_map/ppermute | solution.py:15
  183.6 7.3 %collective-permute-start.37 = (bf16[1,32,96]{2,1,0:T(8,128)(2,1)S(1)}, bf16[1,32,96]{2,1,0:T(8,128)(2,1)S(1)}, u32[]{:S(2)}, u32[]{:S(2)}) collective-permute-start(bf16[1,32,96]{2,1,0:T(8,128)(2,1)S(1)} %get-tuple-element.53), channel_id=1, source_target_pairs={{1,0},{2,1},{3,2},{4,3},{5,4},{6,5},{7,6},{9,8},{10,9},{11,10},{12... | collective-permute-start | bytes 18440 | tf_op jit(solution)/shard_map/ppermute | solution.py:15
  185.5 5.4 %collective-permute-start.38 = (bf16[32,1,96]{2,1,0:T(2,128)(2,1)S(1)}, bf16[32,1,96]{2,1,0:T(2,128)(2,1)S(1)}, u32[]{:S(2)}, u32[]{:S(2)}) collective-permute-start(bf16[32,1,96]{2,1,0:T(2,128)(2,1)S(1)} %get-tuple-element.56), channel_id=1, source_target_pairs={{0,8},{8,16},{16,24},{24,32},{32,40},{40,48},{48,56},{56,64},{64,7... | collective-permute-start | bytes 18440 | tf_op jit(solution)/shard_map/ppermute | solution.py:15
  187.4 7.8 %collective-permute-start.39 = (bf16[32,1,96]{2,1,0:T(2,128)(2,1)S(1)}, bf16[32,1,96]{2,1,0:T(2,128)(2,1)S(1)}, u32[]{:S(2)}, u32[]{:S(2)}) collective-permute-start(bf16[32,1,96]{2,1,0:T(2,128)(2,1)S(1)} %get-tuple-element.57), channel_id=1, source_target_pairs={{8,0},{16,8},{24,16},{32,24},{40,32},{48,40},{56,48},{64,56},{72,6... | collective-permute-start | bytes 18440 | tf_op jit(solution)/shard_map/ppermute | solution.py:15
  196.2 6.7 %collective-permute-start.40 = (bf16[8,32,96]{2,1,0:T(8,128)(2,1)S(1)}, bf16[8,32,96]{2,1,0:T(8,128)(2,1)S(1)}, u32[]{:S(2)}, u32[]{:S(2)}) collective-permute-start(bf16[8,32,96]{2,1,0:T(8,128)(2,1)S(1)} %get-tuple-element.50), channel_id=1, source_target_pairs={{0,1},{1,2},{2,3},{3,4},{4,5},{5,6},{6,7},{8,9},{9,10},{10,11},{11... | collective-permute-start | bytes 147464 | tf_op jit(solution)/shard_map/ppermute | solution.py:15
  201.0 5.6 %collective-permute-start.41 = (bf16[8,32,96]{2,1,0:T(8,128)(2,1)S(1)}, bf16[8,32,96]{2,1,0:T(8,128)(2,1)S(1)}, u32[]{:S(2)}, u32[]{:S(2)}) collective-permute-start(bf16[8,32,96]{2,1,0:T(8,128)(2,1)S(1)} %get-tuple-element.51), channel_id=1, source_target_pairs={{1,0},{2,1},{3,2},{4,3},{5,4},{6,5},{7,6},{9,8},{10,9},{11,10},{12... | collective-permute-start | bytes 147464 | tf_op jit(solution)/shard_map/ppermute | solution.py:15
  206.6 5.5 %collective-permute-start.42 = (bf16[48,8,96]{2,1,0:T(8,128)(2,1)S(1)}, bf16[48,8,96]{2,1,0:T(8,128)(2,1)S(1)}, u32[]{:S(2)}, u32[]{:S(2)}) collective-permute-start(bf16[48,8,96]{2,1,0:T(8,128)(2,1)S(1)} %get-tuple-element.30), channel_id=1, source_target_pairs={{0,8},{8,16},{16,24},{24,32},{32,40},{40,48},{48,56},{56,64},{64,7... | collective-permute-start | bytes 221192 | tf_op jit(solution)/shard_map/ppermute | solution.py:15
  208.6 8.7 %collective-permute-start.43 = (bf16[48,8,96]{2,1,0:T(8,128)(2,1)S(1)}, bf16[48,8,96]{2,1,0:T(8,128)(2,1)S(1)}, u32[]{:S(2)}, u32[]{:S(2)}) collective-permute-start(bf16[48,8,96]{2,1,0:T(8,128)(2,1)S(1)} %get-tuple-element.31), channel_id=1, source_target_pairs={{8,0},{16,8},{24,16},{32,24},{40,32},{48,40},{56,48},{64,56},{72,6... | collective-permute-start | bytes 221192 | tf_op jit(solution)/shard_map/ppermute | solution.py:15
  218.9 14.3 %collective-permute-start.45 = (bf16[1,32,96]{2,1,0:T(8,128)(2,1)S(1)}, bf16[1,32,96]{2,1,0:T(8,128)(2,1)S(1)}, u32[]{:S(2)}, u32[]{:S(2)}) collective-permute-start(bf16[1,32,96]{2,1,0:T(8,128)(2,1)S(1)} %get-tuple-element.48), channel_id=1, source_target_pairs={{1,0},{2,1},{3,2},{4,3},{5,4},{6,5},{7,6},{9,8},{10,9},{11,10},{12... | collective-permute-start | bytes 18440 | tf_op jit(solution)/shard_map/ppermute | solution.py:15
  220.8 12.4 %collective-permute-start.44 = (bf16[1,32,96]{2,1,0:T(8,128)(2,1)S(1)}, bf16[1,32,96]{2,1,0:T(8,128)(2,1)S(1)}, u32[]{:S(2)}, u32[]{:S(2)}) collective-permute-start(bf16[1,32,96]{2,1,0:T(8,128)(2,1)S(1)} %get-tuple-element.49), channel_id=1, source_target_pairs={{0,1},{1,2},{2,3},{3,4},{4,5},{5,6},{6,7},{8,9},{9,10},{10,11},{11... | collective-permute-start | bytes 18440 | tf_op jit(solution)/shard_map/ppermute | solution.py:15
  224.5 8.8 %collective-permute-start.47 = (bf16[32,1,96]{2,1,0:T(2,128)(2,1)S(1)}, bf16[32,1,96]{2,1,0:T(2,128)(2,1)S(1)}, u32[]{:S(2)}, u32[]{:S(2)}) collective-permute-start(bf16[32,1,96]{2,1,0:T(2,128)(2,1)S(1)} %get-tuple-element.44), channel_id=1, source_target_pairs={{8,0},{16,8},{24,16},{32,24},{40,32},{48,40},{56,48},{64,56},{72,6... | collective-permute-start | bytes 18440 | tf_op jit(solution)/shard_map/ppermute | solution.py:15
  226.4 7.5 %collective-permute-start.46 = (bf16[32,1,96]{2,1,0:T(2,128)(2,1)S(1)}, bf16[32,1,96]{2,1,0:T(2,128)(2,1)S(1)}, u32[]{:S(2)}, u32[]{:S(2)}) collective-permute-start(bf16[32,1,96]{2,1,0:T(2,128)(2,1)S(1)} %get-tuple-element.45), channel_id=1, source_target_pairs={{0,8},{8,16},{16,24},{24,32},{32,40},{40,48},{48,56},{56,64},{64,7... | collective-permute-start | bytes 18440 | tf_op jit(solution)/shard_map/ppermute | solution.py:15
  238.0 5.6 %collective-permute-start.49 = (bf16[8,32,96]{2,1,0:T(8,128)(2,1)S(1)}, bf16[8,32,96]{2,1,0:T(8,128)(2,1)S(1)}, u32[]{:S(2)}, u32[]{:S(2)}) collective-permute-start(bf16[8,32,96]{2,1,0:T(8,128)(2,1)S(1)} %get-tuple-element.41), channel_id=1, source_target_pairs={{1,0},{2,1},{3,2},{4,3},{5,4},{6,5},{7,6},{9,8},{10,9},{11,10},{12... | collective-permute-start | bytes 147464 | tf_op jit(solution)/shard_map/ppermute | solution.py:15
  243.6 9.2 %collective-permute-start.50 = (bf16[48,8,96]{2,1,0:T(8,128)(2,1)S(1)}, bf16[48,8,96]{2,1,0:T(8,128)(2,1)S(1)}, u32[]{:S(2)}, u32[]{:S(2)}) collective-permute-start(bf16[48,8,96]{2,1,0:T(8,128)(2,1)S(1)} %get-tuple-element.28), channel_id=1, source_target_pairs={{0,8},{8,16},{16,24},{24,32},{32,40},{40,48},{48,56},{56,64},{64,7... | collective-permute-start | bytes 221192 | tf_op jit(solution)/shard_map/ppermute | solution.py:15
  250.9 8.7 %collective-permute-start.51 = (bf16[48,8,96]{2,1,0:T(8,128)(2,1)S(1)}, bf16[48,8,96]{2,1,0:T(8,128)(2,1)S(1)}, u32[]{:S(2)}, u32[]{:S(2)}) collective-permute-start(bf16[48,8,96]{2,1,0:T(8,128)(2,1)S(1)} %get-tuple-element.29), channel_id=1, source_target_pairs={{8,0},{16,8},{24,16},{32,24},{40,32},{48,40},{56,48},{64,56},{72,6... | collective-permute-start | bytes 221192 | tf_op jit(solution)/shard_map/ppermute | solution.py:15
  (8 other events, 129.7 us)
where the time goes:
time: 265 us; the launch traced here: 263 us
  starting transfers between devices  157 us (59%)
  waiting for transfers between devices  76 us (29%)
  matrix products  11 us (4%)
  other arithmetic  10.5 us (4%)
  local copies, waits for them, and re-layouts  6.21 us (2%)
    ppermute x52, starting transfers between devices, shift_from(): return lax.ppermute(values, axis_name, pair_list)  157 us
    ppermute x52, waiting for transfers between devices, shift_from(): return lax.ppermute(values, axis_name, pair_list)  76 us
    dot_general x6, matrix products, device_fn(): jnp.dot(solve_mat, ext_block.reshape(ext_cells, rhs_count), preferred_ele...  11 us
    convert_element_type x6, other arithmetic, device_fn(): residual.astype(jnp.bfloat16)  6.38 us
  transfers between devices with their start and end apart: 52, of which 21 were waited for; matrix products, arithmetic and copies ran while one was open for 2% of the time, Pallas kernels for 0%

commit v1 on v0

v1 whole, which is shorter than its diff:
```python
import functools
import math
import jax
import jax.numpy as jnp
from jax import lax
from jax.experimental import pallas as pl
from jax.experimental.pallas import tpu as pltpu
from jax.sharding import PartitionSpec as P

SWEEPS = 6
MESH = pl.DeviceIdType.MESH
DIRS = ((-1, 0), (1, 0), (0, -1), (0, 1), (-1, -1), (-1, 1), (1, -1), (1, 1))
BACK = (1, 0, 3, 2, 7, 6, 5, 4)
N, S, W, E, NW, NE, SW, SE = range(8)
F32, BF16 = jnp.float32, jnp.bfloat16


def kernel(geo, omega_ref, f_hbm, u_hbm, k_hbm, a_hbm, out_hbm,
           mat, u, r, ext, zf, cs, cw, ce, kp, kraw, knb,
           ucol, urow_in, ucol_in,
           zo, st_e, st_w, st_c, h_n, h_s, h_w, h_e, h_c,
           load_sem, u_send, u_recv, k_send, k_recv, r_send, r_recv, z_send, z_recv):
    row_count, col_count, sub, halo, rhs = geo
    big = sub + 2 * halo
    tiles = sub // 8
    row, col = lax.axis_index('row'), lax.axis_index('col')
    omega = omega_ref[0, 0]

    def exists(d):
        dr, dc = DIRS[d]
        conds = []
        if dr == -1:
            conds.append(row > 0)
        if dr == 1:
            conds.append(row < row_count - 1)
        if dc == -1:
            conds.append(col > 0)
        if dc == 1:
            conds.append(col < col_count - 1)
        return functools.reduce(jnp.logical_and, conds)

    def device(d):
        dr, dc = DIRS[d]
        return {'row': row + dr, 'col': col + dc}

    def each(fn, dirs=range(8)):
        for d in dirs:
            pl.when(exists(d))(functools.partial(fn, d))

    loads = [pltpu.make_async_copy(k_hbm, kraw, load_sem.at[0]),
             pltpu.make_async_copy(u_hbm, u, load_sem.at[1]),
             pltpu.make_async_copy(f_hbm, r.at[pl.ds(halo, sub), pl.ds(halo, sub)], load_sem.at[2]),
             pltpu.make_async_copy(a_hbm, mat, load_sem.at[3])]
    for copy in loads:
        copy.start()

    for start in (0, halo + sub):
        r[pl.ds(start, halo)] = jnp.zeros((halo, big, rhs), F32)
        r[pl.ds(halo, sub), pl.ds(start, halo)] = jnp.zeros((sub, halo, rhs), F32)
    knb[...] = jnp.zeros_like(knb)

    barrier = pltpu.get_barrier_semaphore()

    def greet(d):
        pl.semaphore_signal(barrier, inc=1, device_id=device(d), device_id_type=MESH)

    each(greet)

    def zero_row(i, carry):
        zf[i] = jnp.zeros((big + 16, rhs), F32)
        return carry

    lax.fori_loop(0, big + 2, zero_row, 0)
    kp[...] = jnp.zeros_like(kp)
    loads[0].wait()
    kp[:, 0:sub] = kraw[...]
    loads[1].wait()

    def u_to_zf(i, carry):
        zf[halo + 1 + i, pl.ds(halo + 8, sub)] = u[pl.ds(pl.multiple_of(i * sub, sub), sub)]
        return carry

    lax.fori_loop(0, sub, u_to_zf, 0)
    ucol[0] = zf[pl.ds(halo + 1, sub), halo + 8, :]
    ucol[1] = zf[pl.ds(halo + 1, sub), halo + 8 + sub - 1, :]

    def band(at, count):
        return 3 - (at == 0).astype(jnp.int32) - (at == count - 1).astype(jnp.int32)

    pl.semaphore_wait(barrier, band(row, row_count) * band(col, col_count) - 1)

    def u_copy(d):
        src = {N: u.at[pl.ds(0, sub)], S: u.at[pl.ds((sub - 1) * sub, sub)],
               W: ucol.at[0], E: ucol.at[1]}[d]
        dst = {N: urow_in.at[1], S: urow_in.at[0], W: ucol_in.at[1], E: ucol_in.at[0]}[d]
        return pltpu.make_async_remote_copy(src, dst, u_send.at[d], u_recv.at[BACK[d]],
                                            device_id=device(d), device_id_type=MESH)

    def u_arrival(d):
        dst = {N: urow_in.at[0], S: urow_in.at[1], W: ucol_in.at[0], E: ucol_in.at[1]}[d]
        return pltpu.make_async_remote_copy(dst, dst, u_send.at[d], u_recv.at[d],
                                            device_id=device(d), device_id_type=MESH)

    def k_copy(d):
        return pltpu.make_async_remote_copy(kp, knb.at[BACK[d]], k_send.at[d], k_recv.at[BACK[d]],
                                            device_id=device(d), device_id_type=MESH)

    def k_arrival(d):
        return pltpu.make_async_remote_copy(knb.at[d], knb.at[d], k_send.at[d], k_recv.at[d],
                                            device_id=device(d), device_id_type=MESH)

    each(lambda d: u_copy(d).start(), (E, W, S, N))
    each(lambda d: k_copy(d).start(), (E, W, S, N, NE, NW, SE, SW))
    each(lambda d: k_arrival(d).wait_recv())

    def block_row(left, mid, right):
        return left + pltpu.roll(mid, sub, 1) + pltpu.roll(right, 2 * sub, 1)

    kk = jnp.concatenate([block_row(knb[NW], knb[N], knb[NE]),
                          block_row(knb[W], kp[...], knb[E]),
                          block_row(knb[SW], knb[S], knb[SE]),
                          jnp.zeros((128 - 3 * sub, 128), F32)], axis=0)
    kt = jnp.transpose(kk)
    g_row = row * sub - sub + lax.broadcasted_iota(jnp.int32, (128, 128), 1)
    g_col = col * sub - sub + lax.broadcasted_iota(jnp.int32, (128, 128), 0)
    row_in = jnp.logical_and(g_row >= 0, g_row < row_count * sub)
    col_in = jnp.logical_and(g_col >= 0, g_col < col_count * sub)
    row_next = jnp.logical_and(g_row >= -1, g_row < row_count * sub - 1)
    col_next = jnp.logical_and(g_col >= -1, g_col < col_count * sub - 1)
    here = jnp.logical_and(row_in, col_in)
    kt = jnp.where(here, kt, 0.0)
    k_down = pltpu.roll(kt, 127, 1)
    k_right = pltpu.roll(kt, 127, 0)
    face_s = jnp.where(jnp.logical_and(here, jnp.logical_and(row_next, col_in)), 0.5, 1.0) * (kt + k_down)
    face_e = jnp.where(jnp.logical_and(here, jnp.logical_and(row_in, col_next)), 0.5, 1.0) * (kt + k_right)
    face_w = pltpu.roll(face_e, 1, 0)
    j0 = sub - halo
    for i in range(-1, big):
        lane = i + sub - halo
        cs[i + 1] = jnp.broadcast_to(face_s[j0:j0 + big, lane:lane + 1], (big, rhs))
        if i >= 0:
            cw[i] = jnp.broadcast_to(face_w[j0:j0 + big, lane:lane + 1], (big, rhs))
            ce[i] = jnp.broadcast_to(face_e[j0:j0 + big, lane:lane + 1], (big, rhs))

    def operator(i, j, width):
        c = zf[i + 1, pl.ds(8 + j, width)]
        span = pl.ds(j, width)
        return (cs[i, span] * (c - zf[i, pl.ds(8 + j, width)])
                + cs[i + 1, span] * (c - zf[i + 2, pl.ds(8 + j, width)])
                + cw[i, span] * (c - zf[i + 1, pl.ds(7 + j, width)])
                + ce[i, span] * (c - zf[i + 1, pl.ds(9 + j, width)]))

    def put_u(d):
        u_arrival(d).wait_recv()
        if d == N:
            zf[halo, pl.ds(halo + 8, sub)] = urow_in[0]
        if d == S:
            zf[halo + sub + 1, pl.ds(halo + 8, sub)] = urow_in[1]
        if d == W:
            zf[pl.ds(halo + 1, sub), halo + 7, :] = ucol_in[0]
        if d == E:
            zf[pl.ds(halo + 1, sub), halo + 8 + sub, :] = ucol_in[1]

    each(put_u, (N, S, W, E))
    loads[2].wait()

    def first_residual(i, carry):
        r[i, pl.ds(halo, sub)] = r[i, pl.ds(halo, sub)] - operator(i, halo, sub)
        return carry

    lax.fori_loop(halo, halo + sub, first_residual, 0)

    def span_of(delta, outer):
        if delta == 0:
            return pl.ds(halo, sub)
        if outer:
            return pl.ds(0, halo) if delta < 0 else pl.ds(halo + sub, halo)
        return pl.ds(halo, halo) if delta < 0 else pl.ds(sub, halo)

    def r_copy(d):
        dr, dc = DIRS[d]
        return pltpu.make_async_remote_copy(
            r.at[span_of(dr, False), span_of(dc, False)], r.at[span_of(-dr, True), span_of(-dc, True)],
            r_send.at[d], r_recv.at[BACK[d]], device_id=device(d), device_id_type=MESH)

    def r_arrival(d):
        dr, dc = DIRS[d]
        dst = r.at[span_of(dr, True), span_of(dc, True)]
        return pltpu.make_async_remote_copy(dst, dst, r_send.at[d], r_recv.at[d],
                                            device_id=device(d), device_id_type=MESH)

    each(lambda d: r_copy(d).start(), (E, W, NE, NW, SE, SW, S, N))
    each(lambda d: u_copy(d).wait_send(), (N, S, W, E))
    each(lambda d: k_copy(d).wait_send())
    loads[3].wait()
    each(lambda d: r_copy(d).wait_send())
    each(lambda d: r_arrival(d).wait_recv())

    def round_row(i, carry):
        ext[i] = r[i].astype(BF16)
        return carry

    lax.fori_loop(0, big, round_row, 0)

    def solve(chunk, e):
        z = jnp.dot(mat[pl.ds(chunk * 8 * sub, 8 * sub), :], e, preferred_element_type=F32)
        return z.astype(BF16).astype(F32)

    def z_source(d, slot):
        return {N: zo.at[slot, pl.ds(0, halo + 1)], S: zo.at[slot, pl.ds(sub - halo - 1, halo + 1)],
                W: st_w.at[slot], E: st_e.at[slot]}.get(d, st_c.at[slot, d - 4] if d >= 4 else None)

    def z_place(d, slot):
        return {N: h_n.at[slot], S: h_s.at[slot], W: h_w.at[slot], E: h_e.at[slot]}.get(
            d, h_c.at[slot, d - 4] if d >= 4 else None)

    def z_copy(d, slot):
        return pltpu.make_async_remote_copy(
            z_source(d, slot), z_place(BACK[d], slot), z_send.at[slot, d], z_recv.at[slot, BACK[d]],
            device_id=device(d), device_id_type=MESH)

    def z_arrival(d, slot):
        return pltpu.make_async_remote_copy(
            z_place(d, slot), z_place(d, slot), z_send.at[slot, d], z_recv.at[slot, d],
            device_id=device(d), device_id_type=MESH)

    left_col, right_col = halo, sub - halo - 1
    low, high = pl.ds(0, halo + 1), pl.ds(sub - halo - 1, halo + 1)

    def sweep(t, carry):
        slot = lax.rem(t, 2)
        e = ext[...].reshape(big * big, rhs)
        for chunk in range(sub // 8):
            z = solve(chunk, e)
            rows = pl.ds(8 * chunk, 8)
            zf[pl.ds(halo + 1 + 8 * chunk, 8), pl.ds(halo + 8, sub)] = z.reshape(8, sub, rhs)
            zb = z.reshape(8, tiles, 8, rhs).astype(BF16)
            zo[slot, rows] = zb
            st_w[slot, rows] = zb[:, 0]
            st_e[slot, rows] = zb[:, tiles - 1]
            st_w[slot, sub + chunk] = zf[pl.ds(halo + 1 + 8 * chunk, 8), halo + 8 + left_col, :].astype(BF16)
            st_e[slot, sub + chunk] = zf[pl.ds(halo + 1 + 8 * chunk, 8), halo + 8 + right_col, :].astype(BF16)
        for d, strip, rows, extra in ((NW, st_w, low, 0), (NE, st_e, low, 0),
                                      (SW, st_w, high, tiles - 1), (SE, st_e, high, tiles - 1)):
            st_c[slot, d - 4, pl.ds(0, halo + 1)] = strip[slot, rows]
            st_c[slot, d - 4, halo + 1] = strip[slot, sub + extra]
        each(lambda d: z_copy(d, slot).start(), (E, W, NE, NW, SE, SW, S, N))

        def add_u(i, c):
            cells = pl.ds(pl.multiple_of(i * sub, sub), sub)
            u[cells] = u[cells] + omega * zf[halo + 1 + i, pl.ds(halo + 8, sub)]
            return c

        lax.fori_loop(0, sub, add_u, 0)
        right, below = halo + sub + 8, halo + sub + 1

        def put_z(d):
            z_arrival(d, slot).wait_recv()
            if d in (N, S):
                buf, at = (h_n, 0) if d == N else (h_s, below)
                zf[pl.ds(at, halo + 1), pl.ds(halo + 8, sub)] = buf[slot].astype(F32).reshape(halo + 1, sub, rhs)
            elif d in (W, E):
                buf, at, edge = (h_w, 8, 7) if d == W else (h_e, right, right + 8)
                zf[pl.ds(halo + 1, sub), pl.ds(at, 8)] = buf[slot, pl.ds(0, sub)].astype(F32)
                for k in range(tiles):
                    zf[pl.ds(halo + 1 + 8 * k, 8), edge, :] = buf[slot, sub + k].astype(F32)
            else:
                dr, dc = DIRS[d]
                at, edge = (8, 7) if dc < 0 else (right, right + 8)
                start, edge_start = (0, 1) if dr < 0 else (below, below)
                zf[pl.ds(start, halo + 1), pl.ds(at, 8)] = h_c[slot, d - 4, pl.ds(0, halo + 1)].astype(F32)
                zf[pl.ds(edge_start, 8), edge, :] = h_c[slot, d - 4, halo + 1].astype(F32)

        each(put_z)

        def update(i, c):
            new = r[i] - omega * operator(i, 0, big)
            r[i] = new
            ext[i] = new.astype(BF16)
            return c

        lax.fori_loop(0, big, update, 0)
        each(lambda d: z_copy(d, slot).wait_send())
        return carry

    lax.fori_loop(0, SWEEPS - 1, sweep, 0)
    e = ext[...].reshape(big * big, rhs)
    for chunk in range(sub // 8):
        cells = pl.ds(chunk * 8 * sub, 8 * sub)
        u[cells] = u[cells] + omega * solve(chunk, e)
    done = pltpu.make_async_copy(u, out_hbm, load_sem.at[0])
    done.start()
    done.wait()


def solution(mesh):
    row_count = mesh.shape['row']
    col_count = mesh.shape['col']
    grid_spec = P('row', 'col', None)

    def device_fn(f_blk, u_blk, kappa_blk, mat_blk, omega_relax):
        sub, _, rhs = u_blk.shape
        rows, cols = mat_blk.shape[2:]
        big = math.isqrt(cols)
        halo = (big - sub) // 2
        tiles = sub // 8
        dma, vmem = pltpu.SemaphoreType.DMA, pltpu.VMEM
        out = pl.pallas_call(
            functools.partial(kernel, (row_count, col_count, sub, halo, rhs)),
            out_shape=jax.ShapeDtypeStruct((sub * sub, rhs), F32),
            in_specs=[pl.BlockSpec(memory_space=pltpu.SMEM)] + [pl.BlockSpec(memory_space=pl.ANY)] * 4,
            out_specs=pl.BlockSpec(memory_space=pl.ANY),
            scratch_shapes=[
                vmem((rows, cols), BF16), vmem((sub * sub, rhs), F32), vmem((big, big, rhs), F32),
                vmem((big, big, rhs), BF16), vmem((big + 2, big + 16, rhs), F32),
                vmem((big + 1, big, rhs), F32), vmem((big, big, rhs), F32), vmem((big, big, rhs), F32),
                vmem((sub, 128), F32), vmem((sub, sub), F32), vmem((8, sub, 128), F32),
                vmem((2, sub, rhs), F32), vmem((2, sub, rhs), F32), vmem((2, sub, rhs), F32),
                vmem((2, sub, tiles, 8, rhs), BF16),
                vmem((2, sub + tiles, 8, rhs), BF16), vmem((2, sub + tiles, 8, rhs), BF16),
                vmem((2, 4, halo + 2, 8, rhs), BF16),
                vmem((2, halo + 1, tiles, 8, rhs), BF16), vmem((2, halo + 1, tiles, 8, rhs), BF16),
                vmem((2, sub + tiles, 8, rhs), BF16), vmem((2, sub + tiles, 8, rhs), BF16),
                vmem((2, 4, halo + 2, 8, rhs), BF16),
                dma((4,)), dma((4,)), dma((4,)), dma((8,)), dma((8,)), dma((8,)), dma((8,)),
                dma((2, 8)), dma((2, 8)),
            ],
            compiler_params=pltpu.CompilerParams(collective_id=0, has_side_effects=True),
        )(omega_relax.reshape(1, 1), f_blk, u_blk.reshape(sub * sub, rhs), kappa_blk, mat_blk.reshape(rows, cols))
        return out.reshape(sub, sub, rhs)

    return jax.shard_map(device_fn, mesh=mesh,
                         in_specs=(grid_spec, grid_spec, P('row', 'col'), P('row', 'col', None, None), P()),
                         out_specs=grid_spec, check_vma=False)
```

time: 265 us -> 69.9 us (0.26)
  starting transfers between devices: 157 us -> 0 us
  waiting for transfers between devices: 76 us -> 0 us
  Pallas kernels: 0 us -> 67.2 us
  matrix products: 11 us -> 0 us
  other arithmetic: 10.5 us -> 0 us
  local copies, waits for them, and re-layouts: 6.21 us -> 1.87 us
    ppermute x52 -> x0, starting transfers between devices: 157 us -> none  [shift_from(): return lax.ppermute(values, axis_name, pair_list)]
    ppermute x52 -> x0, waiting for transfers between devices: 76 us -> none  [shift_from(): return lax.ppermute(values, axis_name, pair_list)]
    pallas_call x0 -> x1, Pallas kernels: none -> 67.2 us  [device_fn(): pl.pallas_call(functools.partial(kernel, (row_count, col_count, sub, halo...]
    dot_general x6 -> x0, matrix products: 11 us -> none  [device_fn(): jnp.dot(solve_mat, ext_block.reshape(ext_cells, rhs_count), preferred_ele...]
    convert_element_type x26 -> x0, other arithmetic: 6.6 us -> none  [the longest x6 6.38 us: device_fn(): residual.astype(jnp.bfloat16)]
    slice x32 -> x0, local copies, waits for them, and re-layouts: 5.99 us -> none  [the longest x5 1.61 us: apply_local(): up_nb = jnp.concatenate([from_above, center[:-1]], axis=0)]
  transfers between devices with their start and end apart: 52 -> 0, of which waited for: 21 -> 0; matrix products, arithmetic and copies ran while one was open for 2% -> 0% of each run, Pallas kernels for 0% -> 0%
where the time goes in v1:
time: 69.9 us; the launch traced here: 69.8 us
  Pallas kernels  67.2 us (96%)
  local copies, waits for them, and re-layouts  1.87 us (3%)
    pallas_call x1, Pallas kernels, device_fn(): pl.pallas_call(functools.partial(kernel, (row_count, col_count, sub, halo...  67.2 us
    unnamed x1, local copies, waits for them, and re-layouts  1.87 us

profile of v1, /device:TPU:121, one launch (start us, length us, event | category | flops | bytes accessed | tf_op | source)
XLA Modules:
  0.0 69.8 jit_solution(3070499013891962074)
XLA Ops:
  0.7 67.2 %shard_map.55 = f32[1024,96]{1,0:T(8,128)} custom-call(f32[1,1]{1,0:T(1,128)} %bitcast.4.omega_ref, f32[32,32,96]{2,1,0:T(8,128)} %f_hbm.1, f32[1024,96]{1,0:T(8,128)} %bitcast.7, f32[32,32]{1,0:T(8,128)} %k_hbm.1, bf16[1024,2304]{1,0:T(8,128)(2,1)} %bitcast.5), custom_call_target="tpu_custom_call" | custom-call | tf_op jit(solution)/shard_map/pallas_call | solution.py:308
  67.9 1.9 %copy.8 = f32[32,32,96]{2,1,0:T(8,128)} copy(f32[32,32,96]{2,1,0:T(8,128)} %bitcast.6) | data formatting | bytes 786432

commit v2 on v1

v2 whole, which is shorter than its diff:
```python
import functools
import math
import jax
import jax.numpy as jnp
from jax import lax
from jax.experimental import pallas as pl
from jax.experimental.pallas import tpu as pltpu
from jax.sharding import PartitionSpec as P

SWEEPS = 6
MESH = pl.DeviceIdType.MESH
DIRS = ((-1, 0), (1, 0), (0, -1), (0, 1), (-1, -1), (-1, 1), (1, -1), (1, 1))
BACK = (1, 0, 3, 2, 7, 6, 5, 4)
N, S, W, E, NW, NE, SW, SE = range(8)
F32, BF16 = jnp.float32, jnp.bfloat16


def kernel(geo, w_hbm, f_hbm, u_hbm, k_hbm, a_hbm, u,
           mat, r, ext, zf, cs, cw, ce, kp, kraw, knb,
           ucol, urow_in, ucol_in, w_smem,
           zo, st, st_c, h_v, h_h, h_c,
           load_sem, u_send, u_recv, k_send, k_recv, r_send, r_recv, z_send, z_recv):
    row_count, col_count, sub, halo, rhs = geo
    big = sub + 2 * halo
    tiles = sub // 8
    row, col = lax.axis_index('row'), lax.axis_index('col')

    def exists(d):
        dr, dc = DIRS[d]
        conds = []
        if dr == -1:
            conds.append(row > 0)
        if dr == 1:
            conds.append(row < row_count - 1)
        if dc == -1:
            conds.append(col > 0)
        if dc == 1:
            conds.append(col < col_count - 1)
        return functools.reduce(jnp.logical_and, conds)

    def device(d):
        dr, dc = DIRS[d]
        return {'row': row + dr, 'col': col + dc}

    def each(fn, dirs=range(8)):
        for d in dirs:
            pl.when(exists(d))(functools.partial(fn, d))

    cells, edge = sub * sub, (halo + 1) * sub
    loads = [pltpu.make_async_copy(k_hbm, kraw, load_sem.at[0]),
             pltpu.make_async_copy(u_hbm, u, load_sem.at[1]),
             pltpu.make_async_copy(f_hbm, r.at[pl.ds(halo, sub), pl.ds(halo, sub)], load_sem.at[2]),
             pltpu.make_async_copy(a_hbm.at[pl.ds(0, edge)], mat.at[pl.ds(0, edge)], load_sem.at[3]),
             pltpu.make_async_copy(a_hbm.at[pl.ds(cells - edge, edge)], mat.at[pl.ds(edge, edge)], load_sem.at[4]),
             pltpu.make_async_copy(a_hbm.at[pl.ds(edge, cells - 2 * edge)], mat.at[pl.ds(2 * edge, cells - 2 * edge)],
                                   load_sem.at[5]),
             pltpu.make_async_copy(w_hbm, w_smem, load_sem.at[6])]
    for copy in loads:
        copy.start()

    for start in (0, halo + sub):
        r[pl.ds(start, halo)] = jnp.zeros((halo, big, rhs), F32)
        r[pl.ds(halo, sub), pl.ds(start, halo)] = jnp.zeros((sub, halo, rhs), F32)
    knb[...] = jnp.zeros_like(knb)
    h_v[:, 1] = jnp.zeros((2,) + h_v.shape[2:], BF16)
    h_h[:, 1] = jnp.zeros((2,) + h_h.shape[2:], BF16)
    h_c[1] = jnp.zeros(h_c.shape[1:], BF16)

    barrier = pltpu.get_barrier_semaphore()

    def greet(d):
        pl.semaphore_signal(barrier, inc=1, device_id=device(d), device_id_type=MESH)

    each(greet)

    def zero_row(i, carry):
        zf[i] = jnp.zeros((big + 16, rhs), F32)
        return carry

    lax.fori_loop(0, big + 2, zero_row, 0)
    kp[...] = jnp.zeros_like(kp)
    loads[0].wait()
    kp[:, 0:sub] = kraw[...]
    loads[1].wait()

    def u_to_zf(i, carry):
        zf[halo + 1 + i, pl.ds(halo + 8, sub)] = u[pl.ds(pl.multiple_of(i * sub, sub), sub)]
        return carry

    lax.fori_loop(0, sub, u_to_zf, 0)
    ucol[0] = zf[pl.ds(halo + 1, sub), halo + 8, :]
    ucol[1] = zf[pl.ds(halo + 1, sub), halo + 8 + sub - 1, :]

    def band(at, count):
        return 3 - (at == 0).astype(jnp.int32) - (at == count - 1).astype(jnp.int32)

    pl.semaphore_wait(barrier, band(row, row_count) * band(col, col_count) - 1)

    def u_copy(d):
        src = {N: u.at[pl.ds(0, sub)], S: u.at[pl.ds((sub - 1) * sub, sub)],
               W: ucol.at[0], E: ucol.at[1]}[d]
        dst = {N: urow_in.at[1], S: urow_in.at[0], W: ucol_in.at[1], E: ucol_in.at[0]}[d]
        return pltpu.make_async_remote_copy(src, dst, u_send.at[d], u_recv.at[BACK[d]],
                                            device_id=device(d), device_id_type=MESH)

    def u_arrival(d):
        dst = {N: urow_in.at[0], S: urow_in.at[1], W: ucol_in.at[0], E: ucol_in.at[1]}[d]
        return pltpu.make_async_remote_copy(dst, dst, u_send.at[d], u_recv.at[d],
                                            device_id=device(d), device_id_type=MESH)

    def k_copy(d):
        return pltpu.make_async_remote_copy(kp, knb.at[BACK[d]], k_send.at[d], k_recv.at[BACK[d]],
                                            device_id=device(d), device_id_type=MESH)

    def k_arrival(d):
        return pltpu.make_async_remote_copy(knb.at[d], knb.at[d], k_send.at[d], k_recv.at[d],
                                            device_id=device(d), device_id_type=MESH)

    each(lambda d: u_copy(d).start(), (E, W, S, N))
    each(lambda d: k_copy(d).start(), (E, W, S, N, NE, NW, SE, SW))
    def block_row(left, mid, right):
        return left + pltpu.roll(mid, sub, 1) + pltpu.roll(right, 2 * sub, 1)

    j0 = sub - halo

    def faces(north, mid, south):
        kk = jnp.concatenate([north, mid, south, jnp.zeros((128 - 3 * sub, 128), F32)], axis=0)
        kt = jnp.transpose(kk)
        g_row = row * sub - sub + lax.broadcasted_iota(jnp.int32, (128, 128), 1)
        g_col = col * sub - sub + lax.broadcasted_iota(jnp.int32, (128, 128), 0)
        row_in = jnp.logical_and(g_row >= 0, g_row < row_count * sub)
        col_in = jnp.logical_and(g_col >= 0, g_col < col_count * sub)
        row_next = jnp.logical_and(g_row >= -1, g_row < row_count * sub - 1)
        col_next = jnp.logical_and(g_col >= -1, g_col < col_count * sub - 1)
        here = jnp.logical_and(row_in, col_in)
        kt = jnp.where(here, kt, 0.0)
        k_down = pltpu.roll(kt, 127, 1)
        k_right = pltpu.roll(kt, 127, 0)
        face_s = jnp.where(jnp.logical_and(here, jnp.logical_and(row_next, col_in)), 0.5, 1.0) * (kt + k_down)
        face_e = jnp.where(jnp.logical_and(here, jnp.logical_and(row_in, col_next)), 0.5, 1.0) * (kt + k_right)
        return face_s, face_e, pltpu.roll(face_e, 1, 0)

    def spread(face, i, j, width):
        lane = i + j0
        return jnp.broadcast_to(face[j0 + j:j0 + j + width, lane:lane + 1], (width, rhs))

    each(lambda d: k_arrival(d).wait_recv(), (N, S, W, E))
    zero = jnp.zeros((sub, 128), F32)
    mid = block_row(knb[W], kp[...], knb[E])
    face_s, face_e, face_w = faces(block_row(zero, knb[N], zero), mid, block_row(zero, knb[S], zero))
    own = pl.ds(halo, sub)
    for i in range(halo - 1, halo + sub):
        cs[i + 1, own] = spread(face_s, i, halo, sub)
        if i >= halo:
            cw[i, own] = spread(face_w, i, halo, sub)
            ce[i, own] = spread(face_e, i, halo, sub)

    def operator(i, j, width):
        c = zf[i + 1, pl.ds(8 + j, width)]
        span = pl.ds(j, width)
        return (cs[i, span] * (c - zf[i, pl.ds(8 + j, width)])
                + cs[i + 1, span] * (c - zf[i + 2, pl.ds(8 + j, width)])
                + cw[i, span] * (c - zf[i + 1, pl.ds(7 + j, width)])
                + ce[i, span] * (c - zf[i + 1, pl.ds(9 + j, width)]))

    def put_u(d):
        u_arrival(d).wait_recv()
        if d == N:
            zf[halo, pl.ds(halo + 8, sub)] = urow_in[0]
        if d == S:
            zf[halo + sub + 1, pl.ds(halo + 8, sub)] = urow_in[1]
        if d == W:
            zf[pl.ds(halo + 1, sub), halo + 7, :] = ucol_in[0]
        if d == E:
            zf[pl.ds(halo + 1, sub), halo + 8 + sub, :] = ucol_in[1]

    each(put_u, (N, S, W, E))
    loads[2].wait()

    def first_residual(i, carry):
        r[i, pl.ds(halo, sub)] = r[i, pl.ds(halo, sub)] - operator(i, halo, sub)
        return carry

    lax.fori_loop(halo, halo + sub, first_residual, 0, unroll=4)

    def span_of(delta, outer):
        if delta == 0:
            return pl.ds(halo, sub)
        if outer:
            return pl.ds(0, halo) if delta < 0 else pl.ds(halo + sub, halo)
        return pl.ds(halo, halo) if delta < 0 else pl.ds(sub, halo)

    def r_copy(d):
        dr, dc = DIRS[d]
        return pltpu.make_async_remote_copy(
            r.at[span_of(dr, False), span_of(dc, False)], r.at[span_of(-dr, True), span_of(-dc, True)],
            r_send.at[d], r_recv.at[BACK[d]], device_id=device(d), device_id_type=MESH)

    def r_arrival(d):
        dr, dc = DIRS[d]
        dst = r.at[span_of(dr, True), span_of(dc, True)]
        return pltpu.make_async_remote_copy(dst, dst, r_send.at[d], r_recv.at[d],
                                            device_id=device(d), device_id_type=MESH)

    depth = halo + 1
    near, far = pl.ds(0, depth), pl.ds(sub - depth, depth)
    part = {1: pl.ds(0, depth), 2: pl.ds(sub + tiles - depth, depth), 3: pl.ds(depth, sub + tiles - 2 * depth)}
    col_at = sub - depth

    def strip_row(i):
        return i if i < sub - depth else i + tiles

    def z_source(d, k, slot):
        if d in (N, S):
            return zo.at[d, slot]
        return st.at[d - W, slot, part[k]] if d in (W, E) else st_c.at[slot, d - NW]

    def z_place(d, k, slot):
        if d in (N, S):
            return h_v.at[d, slot]
        return h_h.at[d - W, slot, part[k]] if d in (W, E) else h_c.at[slot, d - NW]

    def z_copy(d, k, slot):
        return pltpu.make_async_remote_copy(
            z_source(d, k, slot), z_place(BACK[d], k, slot), z_send.at[slot, k, d], z_recv.at[slot, k, BACK[d]],
            device_id=device(d), device_id_type=MESH)

    def z_arrival(d, k, slot):
        return pltpu.make_async_remote_copy(
            z_place(d, k, slot), z_place(d, k, slot), z_send.at[slot, k, d], z_recv.at[slot, k, d],
            device_id=device(d), device_id_type=MESH)

    def ks(d):
        return (1, 2, 3) if d in (W, E) else (0,)

    left_col, right_col = halo, sub - depth
    chunks = ((0, depth), (sub - depth, depth), (depth, sub - 2 * depth))

    def stage(slot, lo, count, value, column):
        tile = value.reshape(count, tiles, 8, rhs).astype(BF16)
        at = pl.ds(strip_row(lo), count)
        st[0, slot, at] = tile[:, 0]
        st[1, slot, at] = tile[:, tiles - 1]
        if lo == 0:
            zo[N, slot] = tile
            groups, corners = (0,), (NW, NE)
        elif lo == sub - depth:
            zo[S, slot] = tile
            groups, corners = (tiles - 1,), (SW, SE)
        else:
            groups, corners = range(1, tiles - 1), ()
        for k in groups:
            st[0, slot, col_at + k] = column(8 * k, left_col).astype(BF16)
            st[1, slot, col_at + k] = column(8 * k, right_col).astype(BF16)
        for d in corners:
            side = d & 1
            st_c[slot, d - NW, pl.ds(0, depth)] = tile[:, side * (tiles - 1)]
            st_c[slot, d - NW, depth] = st[side, slot, col_at + groups[0]]

    def send(slot, los):
        dirs = []
        if 0 in los:
            dirs += [(NE, 0), (NW, 0)]
        if sub - depth in los:
            dirs += [(SE, 0), (SW, 0)]
        if 0 in los:
            dirs += [(N, 0), (E, 1), (W, 1)]
        if sub - depth in los:
            dirs += [(S, 0), (E, 2), (W, 2)]
        if depth in los:
            dirs += [(E, 3), (W, 3)]
        for d, k in dirs:
            pl.when(exists(d))(lambda: z_copy(d, k, slot).start())

    def sent(slot):
        each(lambda d: [z_copy(d, k, slot).wait_send() for k in ks(d)] and None)

    for lo, count in chunks:
        stage(1, lo, count, r[pl.ds(halo + lo, count), own],
              lambda i, j: r[pl.ds(halo + i, 8), halo + j, :])
    send(1, [lo for lo, _ in chunks])
    each(lambda d: r_copy(d).start(), (NE, NW, SE, SW, E, W, S, N))
    each(lambda d: u_copy(d).wait_send(), (N, S, W, E))
    each(lambda d: k_copy(d).wait_send())
    each(lambda d: k_arrival(d).wait_recv(), (NW, NE, SW, SE))
    face_s, face_e, face_w = faces(block_row(knb[NW], knb[N], knb[NE]), mid, block_row(knb[SW], knb[S], knb[SE]))
    for i in range(-1, big):
        inside = halo <= i < halo + sub
        for j, width in ((0, halo), (halo + sub, halo)) if inside else ((0, big),):
            span = pl.ds(j, width)
            if i == halo - 1:
                cs[i + 1, pl.ds(0, halo)] = spread(face_s, i, 0, halo)
                cs[i + 1, pl.ds(halo + sub, halo)] = spread(face_s, i, halo + sub, halo)
            else:
                cs[i + 1, span] = spread(face_s, i, j, width)
            if i >= 0:
                cw[i, span] = spread(face_w, i, j, width)
                ce[i, span] = spread(face_e, i, j, width)
    for copy in loads[3:]:
        copy.wait()
    omega = w_smem[0, 0]
    each(lambda d: [z_arrival(d, k, 1).wait_recv() for k in ks(d)] and None)
    for i in range(big):
        if i < halo:
            left, mid_r, right = h_c[1, 0, i + 1], h_v[N, 1, i + 1], h_c[1, 1, i + 1]
            mid_r = mid_r.astype(F32).reshape(sub, rhs)
        elif i < halo + sub:
            k = strip_row(i - halo)
            left, mid_r, right = h_h[0, 1, k], r[i, own], h_h[1, 1, k]
        else:
            k = i - halo - sub
            left, mid_r, right = h_c[1, 2, k], h_v[S, 1, k], h_c[1, 3, k]
            mid_r = mid_r.astype(F32).reshape(sub, rhs)
        ext[i] = jnp.concatenate([left.astype(F32), mid_r, right.astype(F32)], axis=0).astype(BF16)
    sent(1)

    k_half = 5 * 256

    def solve(group, e):
        if group == 0:
            parts = [jnp.dot(mat[pl.ds(at, edge), :], e, preferred_element_type=F32) for at in (0, edge)]
        else:
            rows = pl.ds(2 * edge, cells - 2 * edge)
            parts = [jnp.dot(mat[rows, :k_half], e[:k_half], preferred_element_type=F32)
                     + jnp.dot(mat[rows, k_half:], e[k_half:], preferred_element_type=F32)]
        parts = [z.astype(BF16).astype(F32) for z in parts]
        if group == 0:
            return (0, depth, parts[0]), (sub - depth, depth, parts[1])
        return ((depth, sub - 2 * depth, parts[0]),)

    def update(i, j, width):
        span = pl.ds(j, width)
        new = r[i, span] - omega * operator(i, j, width)
        r[i, span] = new
        ext[i, span] = new.astype(BF16)

    def sweep(t, carry):
        slot = lax.rem(t, 2)
        e = ext[...].reshape(big * big, rhs)
        for group in range(2):
            done = solve(group, e)
            for lo, count, z in done:
                z = z.reshape(count, sub, rhs)
                zf[pl.ds(halo + 1 + lo, count), pl.ds(halo + 8, sub)] = z
                stage(slot, lo, count, z, lambda i, j: zf[pl.ds(halo + 1 + i, 8), halo + 8 + j, :])
            send(slot, [lo for lo, _, _ in done])

        for i in range(sub):
            cells = pl.ds(i * sub, sub)
            u[cells] = u[cells] + omega * zf[halo + 1 + i, pl.ds(halo + 8, sub)]

        def r_ready(d):
            r_copy(d).wait_send()
            r_arrival(d).wait_recv()

        @pl.when(t == 0)
        def _():
            each(r_ready)

        for i in range(halo + 1, halo + sub - 1):
            update(i, 16, 16)

        right, below = halo + sub + 8, halo + sub + 1

        def put_z(d):
            for k in ks(d):
                z_arrival(d, k, slot).wait_recv()
            if d in (N, S):
                at = 0 if d == N else below
                zf[pl.ds(at, depth), pl.ds(halo + 8, sub)] = h_v[d, slot].astype(F32).reshape(depth, sub, rhs)
            elif d in (W, E):
                at, edge = (8, 7) if d == W else (right, right + 8)
                for lo, count in chunks:
                    zf[pl.ds(halo + 1 + lo, count), pl.ds(at, 8)] = h_h[d - W, slot, pl.ds(strip_row(lo), count)].astype(F32)
                for k in range(tiles):
                    zf[pl.ds(halo + 1 + 8 * k, 8), edge, :] = h_h[d - W, slot, col_at + k].astype(F32)
            else:
                dr, dc = DIRS[d]
                at, edge = (8, 7) if dc < 0 else (right, right + 8)
                start, edge_start = (0, 1) if dr < 0 else (below, below)
                zf[pl.ds(start, depth), pl.ds(at, 8)] = h_c[slot, d - NW, pl.ds(0, depth)].astype(F32)
                zf[pl.ds(edge_start, 8), edge, :] = h_c[slot, d - NW, depth].astype(F32)

        each(put_z, (N, S))
        for i in (*range(halo + 1), *range(halo + sub - 1, big)):
            update(i, 16, 16)

        def side(d):
            each(put_z, (NW, SW, W) if d == W else (NE, SE, E))
            for i in range(big):
                update(i, 0 if d == W else 32, 16)

        west_last = lax.rem(col, 4) == 0

        @pl.when(west_last)
        def _():
            side(E)
            side(W)

        @pl.when(jnp.logical_not(west_last))
        def _():
            side(W)
            side(E)

        sent(slot)
        return carry

    lax.fori_loop(0, SWEEPS - 1, sweep, 0)
    e = ext[...].reshape(big * big, rhs)
    for group in range(2):
        for lo, count, z in solve(group, e):
            span = pl.ds(lo * sub, count * sub)
            u[span] = u[span] + omega * z


def write_out(u_ref, out_hbm, sem):
    copy = pltpu.make_async_copy(u_ref, out_hbm, sem)
    copy.start()
    copy.wait()


def solution(mesh):
    row_count = mesh.shape['row']
    col_count = mesh.shape['col']
    grid_spec = P('row', 'col', None)

    def device_fn(f_blk, u_blk, kappa_blk, mat_blk, omega_relax):
        sub, _, rhs = u_blk.shape
        rows, cols = mat_blk.shape[2:]
        big = math.isqrt(cols)
        halo = (big - sub) // 2
        tiles = sub // 8
        dma, vmem = pltpu.SemaphoreType.DMA, pltpu.VMEM
        flat = jax.ShapeDtypeStruct((sub * sub, rhs), F32)
        u_new = pl.pallas_call(
            functools.partial(kernel, (row_count, col_count, sub, halo, rhs)),
            out_shape=pltpu.VMEM(flat.shape, F32),
            in_specs=[pl.BlockSpec(memory_space=pl.ANY)] * 5,
            out_specs=pl.BlockSpec(memory_space=pltpu.VMEM),
            scratch_shapes=[
                vmem((rows, cols), BF16), vmem((big, big, rhs), F32),
                vmem((big, big, rhs), BF16), vmem((big + 2, big + 16, rhs), F32),
                vmem((big + 1, big, rhs), F32), vmem((big, big, rhs), F32), vmem((big, big, rhs), F32),
                vmem((sub, 128), F32), vmem((sub, sub), F32), vmem((8, sub, 128), F32),
                vmem((2, sub, rhs), F32), vmem((2, sub, rhs), F32), vmem((2, sub, rhs), F32),
                pltpu.SMEM((1, 1), F32),
                vmem((2, 2, halo + 1, tiles, 8, rhs), BF16), vmem((2, 2, sub + tiles, 8, rhs), BF16),
                vmem((2, 4, halo + 2, 8, rhs), BF16),
                vmem((2, 2, halo + 1, tiles, 8, rhs), BF16), vmem((2, 2, sub + tiles, 8, rhs), BF16),
                vmem((2, 4, halo + 2, 8, rhs), BF16),
                dma((7,)), dma((4,)), dma((4,)), dma((8,)), dma((8,)), dma((8,)), dma((8,)),
                dma((2, 4, 8)), dma((2, 4, 8)),
            ],
            compiler_params=pltpu.CompilerParams(collective_id=0, has_side_effects=True),
        )(omega_relax.reshape(1, 1), f_blk, u_blk.reshape(sub * sub, rhs), kappa_blk, mat_blk.reshape(rows, cols))
        out = pl.pallas_call(
            write_out, out_shape=flat,
            in_specs=[pl.BlockSpec(memory_space=pltpu.VMEM)], out_specs=pl.BlockSpec(memory_space=pl.ANY),
            scratch_shapes=[dma],
        )(u_new)
        return out.reshape(sub, sub, rhs)

    return jax.shard_map(device_fn, mesh=mesh,
                         in_specs=(grid_spec, grid_spec, P('row', 'col'), P('row', 'col', None, None), P()),
                         out_specs=grid_spec, check_vma=False)
```

time: 69.9 us -> 57.6 us (0.82)
  Pallas kernels: 67.2 us -> 55.3 us
  local copies, waits for them, and re-layouts: 1.87 us -> 0.78 us
    pallas_call x1, Pallas kernels: 67.2 us -> 53.5 us  [device_fn(): pl.pallas_call(functools.partial(kernel, (row_count, col_count, sub, halo...]
    pallas_call x0 -> x1, Pallas kernels: none -> 1.84 us  [device_fn(): pl.pallas_call(write_out, out_shape=flat, in_specs=[pl.BlockSpec(memory_s...]
    unnamed x1 -> x2, local copies, waits for them, and re-layouts: 1.87 us -> 0.78 us
where the time goes in v2:
time: 57.6 us; the launch traced here: 56.8 us
  Pallas kernels  55.3 us (96%)
  local copies, waits for them, and re-layouts  0.78 us (1%)
  between operations  0.67 us (1%)
    pallas_call x1, Pallas kernels, device_fn(): pl.pallas_call(functools.partial(kernel, (row_count, col_count, sub, halo...  53.5 us
    pallas_call x1, Pallas kernels, device_fn(): pl.pallas_call(write_out, out_shape=flat, in_specs=[pl.BlockSpec(memory_s...  1.84 us

profile of v2, /device:TPU:121, one launch (start us, length us, event | category | flops | bytes accessed | tf_op | source)
XLA Modules:
  0.0 56.8 jit_solution(12958856196810738591)
XLA Ops:
  0.7 53.5 %shard_map.55.u_ref = f32[1024,96]{1,0:T(8,128)S(1)} custom-call(f32[1,1]{1,0:T(1,128)} %bitcast.4.w_hbm, f32[32,32,96]{2,1,0:T(8,128)} %f_hbm.1, f32[1024,96]{1,0:T(8,128)} %bitcast.6, f32[32,32]{1,0:T(8,128)} %k_hbm.1, bf16[1024,2304]{1,0:T(8,128)(2,1)} %bitcast.5), custom_call_target="tpu_custom_call" | custom-call | tf_op jit(solution)/shard_map/pallas_call | solution.py:435
  54.2 0.0 copy-start
  54.2 0.8 %copy-done = f32[1024,96]{1,0:T(8,128)} copy-done((f32[1024,96]{1,0:T(8,128)}, f32[1024,96]{1,0:T(8,128)S(1)}, u32[]{:S(2)}) %copy-start) | copy-done | bytes 393240
  54.9 1.8 %shard_map.56 = f32[1024,96]{1,0:T(8,128)} custom-call(f32[1024,96]{1,0:T(8,128)} %copy-done), custom_call_target="tpu_custom_call" | custom-call | tf_op jit(solution)/shard_map/pallas_call | solution.py:456
Async XLA Ops:
  54.2 0.8 %copy-start = (f32[1024,96]{1,0:T(8,128)}, f32[1024,96]{1,0:T(8,128)S(1)}, u32[]{:S(2)}) copy-start(f32[1024,96]{1,0:T(8,128)S(1)} %shard_map.55.u_ref) | copy-start | bytes 1179652

commit v3 on v2

--- a/solution.py
+++ b/solution.py
@@ -15,10 +15,10 @@
 F32, BF16 = jnp.float32, jnp.bfloat16
 
 
-def kernel(geo, w_hbm, f_hbm, u_hbm, k_hbm, a_hbm, u,
+def kernel(geo, w_hbm, f_hbm, u_hbm, k_hbm, a_hbm, u, z_last,
            mat, r, ext, zf, cs, cw, ce, kp, kraw, knb,
            ucol, urow_in, ucol_in, w_smem,
-           zo, st, st_c, h_v, h_h, h_c,
+           zo, st_a, st_b, st_c, h_v, h_a, h_b, h_c,
            load_sem, u_send, u_recv, k_send, k_recv, r_send, r_recv, z_send, z_recv):
     row_count, col_count, sub, halo, rhs = geo
     big = sub + 2 * halo
@@ -63,7 +63,9 @@
         r[pl.ds(halo, sub), pl.ds(start, halo)] = jnp.zeros((sub, halo, rhs), F32)
     knb[...] = jnp.zeros_like(knb)
     h_v[:, 1] = jnp.zeros((2,) + h_v.shape[2:], BF16)
-    h_h[:, 1] = jnp.zeros((2,) + h_h.shape[2:], BF16)
+    h_a[:, 1] = jnp.zeros((2,) + h_a.shape[2:], BF16)
+    h_b[:, 1] = jnp.zeros((2,) + h_b.shape[2:], BF16)
+    st_c[...] = jnp.zeros_like(st_c)
     h_c[1] = jnp.zeros(h_c.shape[1:], BF16)
 
     barrier = pltpu.get_barrier_semaphore()
@@ -83,13 +85,8 @@
     kp[:, 0:sub] = kraw[...]
     loads[1].wait()
 
-    def u_to_zf(i, carry):
-        zf[halo + 1 + i, pl.ds(halo + 8, sub)] = u[pl.ds(pl.multiple_of(i * sub, sub), sub)]
-        return carry
-
-    lax.fori_loop(0, sub, u_to_zf, 0)
-    ucol[0] = zf[pl.ds(halo + 1, sub), halo + 8, :]
-    ucol[1] = zf[pl.ds(halo + 1, sub), halo + 8 + sub - 1, :]
+    ucol[0] = u[pl.ds(0, sub, stride=sub)]
+    ucol[1] = u[pl.ds(sub - 1, sub, stride=sub)]
 
     def band(at, count):
         return 3 - (at == 0).astype(jnp.int32) - (at == count - 1).astype(jnp.int32)
@@ -118,6 +115,12 @@
 
     each(lambda d: u_copy(d).start(), (E, W, S, N))
     each(lambda d: k_copy(d).start(), (E, W, S, N, NE, NW, SE, SW))
+
+    def u_to_zf(i, carry):
+        zf[halo + 1 + i, pl.ds(halo + 8, sub)] = u[pl.ds(pl.multiple_of(i * sub, sub), sub)]
+        return carry
+
+    lax.fori_loop(0, sub, u_to_zf, 0, unroll=8)
     def block_row(left, mid, right):
         return left + pltpu.roll(mid, sub, 1) + pltpu.roll(right, 2 * sub, 1)
 
@@ -144,16 +147,14 @@
         lane = i + j0
         return jnp.broadcast_to(face[j0 + j:j0 + j + width, lane:lane + 1], (width, rhs))
 
-    each(lambda d: k_arrival(d).wait_recv(), (N, S, W, E))
     zero = jnp.zeros((sub, 128), F32)
-    mid = block_row(knb[W], kp[...], knb[E])
-    face_s, face_e, face_w = faces(block_row(zero, knb[N], zero), mid, block_row(zero, knb[S], zero))
     own = pl.ds(halo, sub)
-    for i in range(halo - 1, halo + sub):
-        cs[i + 1, own] = spread(face_s, i, halo, sub)
-        if i >= halo:
-            cw[i, own] = spread(face_w, i, halo, sub)
-            ce[i, own] = spread(face_e, i, halo, sub)
+    face_s, face_e, face_w = faces(zero, block_row(zero, kp[...], zero), zero)
+    for i in range(halo, halo + sub):
+        if i < halo + sub - 1:
+            cs[i + 1, own] = spread(face_s, i, halo, sub)
+        cw[i, own] = spread(face_w, i, halo, sub)
+        ce[i, own] = spread(face_e, i, halo, sub)
 
     def operator(i, j, width):
         c = zf[i + 1, pl.ds(8 + j, width)]
@@ -174,14 +175,29 @@
         if d == E:
             zf[pl.ds(halo + 1, sub), halo + 8 + sub, :] = ucol_in[1]
 
+    loads[2].wait()
+
+    def first_residual(i, j, width):
+        span = pl.ds(j, width)
+        r[i, span] = r[i, span] - operator(i, j, width)
+
+    for i in range(halo + 1, halo + sub - 1):
+        first_residual(i, 16, 16)
+    each(lambda d: k_arrival(d).wait_recv(), (N, S, W, E))
+    mid = block_row(knb[W], kp[...], knb[E])
+    face_s, face_e, face_w = faces(block_row(zero, knb[N], zero), mid, block_row(zero, knb[S], zero))
+    for i in (halo - 1, halo + sub - 1):
+        cs[i + 1, own] = spread(face_s, i, halo, sub)
+    for i in range(halo, halo + sub):
+        cw[i, pl.ds(halo, 8)] = spread(face_w, i, halo, 8)
+        ce[i, pl.ds(halo + sub - 8, 8)] = spread(face_e, i, halo + sub - 8, 8)
     each(put_u, (N, S, W, E))
-    loads[2].wait()
-
-    def first_residual(i, carry):
-        r[i, pl.ds(halo, sub)] = r[i, pl.ds(halo, sub)] - operator(i, halo, sub)
-        return carry
-
-    lax.fori_loop(halo, halo + sub, first_residual, 0, unroll=4)
+    for i in range(halo, halo + sub):
+        if i in (halo, halo + sub - 1):
+            first_residual(i, halo, sub)
+        else:
+            first_residual(i, halo, 8)
+            first_residual(i, halo + sub - 8, 8)
 
     def span_of(delta, outer):
         if delta == 0:
@@ -203,22 +219,29 @@
                                             device_id=device(d), device_id_type=MESH)
 
     depth = halo + 1
-    near, far = pl.ds(0, depth), pl.ds(sub - depth, depth)
-    part = {1: pl.ds(0, depth), 2: pl.ds(sub + tiles - depth, depth), 3: pl.ds(depth, sub + tiles - 2 * depth)}
-    col_at = sub - depth
-
-    def strip_row(i):
-        return i if i < sub - depth else i + tiles
+    left_col, right_col = halo, sub - depth
+    chunks = ((0, depth), (sub - depth, depth), (depth, sub - 2 * depth))
+    lanes = 128 - rhs
+
+    def pack(tile):
+        t = tile.reshape(tile.shape[0] // 4, 4, 8, rhs)
+        last = jnp.stack([t[:, 3, :, k * lanes:(k + 1) * lanes] for k in range(3)], axis=1)
+        return jnp.concatenate([t[:, :3], last], axis=-1).reshape(-1, 8, 128).astype(BF16)
+
+    def unpack(packed):
+        p = packed.astype(F32).reshape(-1, 3, 8, 128)
+        last = jnp.concatenate([p[:, k, :, rhs:] for k in range(3)], axis=-1)
+        return jnp.concatenate([p[:, :, :, :rhs], last[:, None]], axis=1).reshape(-1, 8, rhs)
 
     def z_source(d, k, slot):
         if d in (N, S):
             return zo.at[d, slot]
-        return st.at[d - W, slot, part[k]] if d in (W, E) else st_c.at[slot, d - NW]
+        return (st_a, st_b)[k].at[d - W, slot] if d in (W, E) else st_c.at[slot, d - NW]
 
     def z_place(d, k, slot):
         if d in (N, S):
             return h_v.at[d, slot]
-        return h_h.at[d - W, slot, part[k]] if d in (W, E) else h_c.at[slot, d - NW]
+        return (h_a, h_b)[k].at[d - W, slot] if d in (W, E) else h_c.at[slot, d - NW]
 
     def z_copy(d, k, slot):
         return pltpu.make_async_remote_copy(
@@ -231,54 +254,61 @@
             device_id=device(d), device_id_type=MESH)
 
     def ks(d):
-        return (1, 2, 3) if d in (W, E) else (0,)
-
-    left_col, right_col = halo, sub - depth
-    chunks = ((0, depth), (sub - depth, depth), (depth, sub - 2 * depth))
-
-    def stage(slot, lo, count, value, column):
-        tile = value.reshape(count, tiles, 8, rhs).astype(BF16)
-        at = pl.ds(strip_row(lo), count)
-        st[0, slot, at] = tile[:, 0]
-        st[1, slot, at] = tile[:, tiles - 1]
-        if lo == 0:
-            zo[N, slot] = tile
-            groups, corners = (0,), (NW, NE)
-        elif lo == sub - depth:
-            zo[S, slot] = tile
-            groups, corners = (tiles - 1,), (SW, SE)
-        else:
-            groups, corners = range(1, tiles - 1), ()
-        for k in groups:
-            st[0, slot, col_at + k] = column(8 * k, left_col).astype(BF16)
-            st[1, slot, col_at + k] = column(8 * k, right_col).astype(BF16)
-        for d in corners:
-            side = d & 1
-            st_c[slot, d - NW, pl.ds(0, depth)] = tile[:, side * (tiles - 1)]
-            st_c[slot, d - NW, depth] = st[side, slot, col_at + groups[0]]
-
-    def send(slot, los):
-        dirs = []
-        if 0 in los:
-            dirs += [(NE, 0), (NW, 0)]
-        if sub - depth in los:
-            dirs += [(SE, 0), (SW, 0)]
-        if 0 in los:
-            dirs += [(N, 0), (E, 1), (W, 1)]
-        if sub - depth in los:
-            dirs += [(S, 0), (E, 2), (W, 2)]
-        if depth in los:
-            dirs += [(E, 3), (W, 3)]
-        for d, k in dirs:
+        return (0, 1) if d in (W, E) else (0,)
+
+    def start(slot, messages):
+        for d, k in messages:
             pl.when(exists(d))(lambda: z_copy(d, k, slot).start())
+
+    def stage_ends(slot, near, far, column):
+        for side, (d_near, d_far) in enumerate(((NW, SW), (NE, SE))):
+            cells8 = slice(side * (sub - 8), side * (sub - 8) + 8)
+            t_near, t_far = near[:, cells8], far[:, cells8]
+            j = (left_col, right_col)[side]
+            extra = (t_near[halo:], t_far[:1], column(0, j)[None], column(sub - 8, j)[None])
+            packed = pack(jnp.concatenate([t_near[:halo], t_far[1:], *extra], axis=0))
+            third = 3 * halo // 4
+            st_a[side, slot] = packed
+            for d, at, raw in ((d_near, 0, (0, 2)), (d_far, third, (1, 3))):
+                st_c[slot, d - NW, pl.ds(0, third)] = packed[at:at + third]
+                for n, k in enumerate(raw):
+                    st_c[slot, d - NW, third + n, :, pl.ds(0, rhs)] = extra[k][0].astype(BF16)
+        zo[N, slot] = near.reshape(depth, tiles, 8, rhs).astype(BF16)
+        zo[S, slot] = far.reshape(depth, tiles, 8, rhs).astype(BF16)
+        start(slot, ((NE, 0), (NW, 0), (SE, 0), (SW, 0), (E, 0), (W, 0), (N, 0), (S, 0)))
+
+    def stage_middle(slot, middle, column):
+        for side in range(2):
+            j = (left_col, right_col)[side]
+            inner = [column(8 * k, j)[None] for k in range(1, tiles - 1)]
+            st_b[side, slot] = pack(jnp.concatenate([middle[:, side * (sub - 8):side * (sub - 8) + 8], *inner], axis=0))
+        start(slot, ((E, 1), (W, 1)))
+
+    def strip_parts(side, slot):
+        a, b = unpack(h_a[side, slot]), unpack(h_b[side, slot])
+        inner = sub - 2 * depth
+        rows = [(0, a[:halo]), (halo, a[2 * halo:2 * halo + 1]), (depth, b[:inner]),
+                (sub - depth, a[2 * halo + 1:2 * halo + 2]), (sub - halo, a[halo:2 * halo])]
+        cols = [(0, a[2 * halo + 2]), (sub - 8, a[2 * halo + 3])]
+        cols += [(8 * k, b[inner + k - 1]) for k in range(1, tiles - 1)]
+        return rows, cols
+
+    def corner_parts(d, slot):
+        third = 3 * halo // 4
+        rows = unpack(h_c[slot, d - NW, pl.ds(0, third)])
+        row, column = [h_c[slot, d - NW, third + n, :, pl.ds(0, rhs)].astype(F32) for n in range(2)]
+        return jnp.concatenate([row[None], rows] if d in (NW, NE) else [rows, row[None]], axis=0), column
 
     def sent(slot):
         each(lambda d: [z_copy(d, k, slot).wait_send() for k in ks(d)] and None)
 
-    for lo, count in chunks:
-        stage(1, lo, count, r[pl.ds(halo + lo, count), own],
-              lambda i, j: r[pl.ds(halo + i, 8), halo + j, :])
-    send(1, [lo for lo, _ in chunks])
+    near_r, far_r, middle_r = [r[pl.ds(halo + lo, count), own] for lo, count in chunks]
+
+    def r_column(i, j):
+        return r[pl.ds(halo + i, 8), halo + j, :]
+
+    stage_ends(1, near_r, far_r, r_column)
+    stage_middle(1, middle_r, r_column)
     each(lambda d: r_copy(d).start(), (NE, NW, SE, SW, E, W, S, N))
     each(lambda d: u_copy(d).wait_send(), (N, S, W, E))
     each(lambda d: k_copy(d).wait_send())
@@ -300,33 +330,30 @@
         copy.wait()
     omega = w_smem[0, 0]
     each(lambda d: [z_arrival(d, k, 1).wait_recv() for k in ks(d)] and None)
+    strips = [strip_parts(side, 1)[0] for side in range(2)]
+    strips = [jnp.concatenate([t for _, t in rows], axis=0) for rows in strips]
+    corner = {d: corner_parts(d, 1)[0] for d in (NW, NE, SW, SE)}
     for i in range(big):
         if i < halo:
-            left, mid_r, right = h_c[1, 0, i + 1], h_v[N, 1, i + 1], h_c[1, 1, i + 1]
-            mid_r = mid_r.astype(F32).reshape(sub, rhs)
+            left, right = corner[NW][i + 1], corner[NE][i + 1]
+            middle = h_v[N, 1, i + 1].astype(F32).reshape(sub, rhs)
         elif i < halo + sub:
-            k = strip_row(i - halo)
-            left, mid_r, right = h_h[0, 1, k], r[i, own], h_h[1, 1, k]
+            left, middle, right = strips[0][i - halo], r[i, own], strips[1][i - halo]
         else:
             k = i - halo - sub
-            left, mid_r, right = h_c[1, 2, k], h_v[S, 1, k], h_c[1, 3, k]
-            mid_r = mid_r.astype(F32).reshape(sub, rhs)
-        ext[i] = jnp.concatenate([left.astype(F32), mid_r, right.astype(F32)], axis=0).astype(BF16)
+            left, right = corner[SW][k], corner[SE][k]
+            middle = h_v[S, 1, k].astype(F32).reshape(sub, rhs)
+        ext[i] = jnp.concatenate([left, middle, right], axis=0).astype(BF16)
     sent(1)
 
-    k_half = 5 * 256
-
-    def solve(group, e):
-        if group == 0:
-            parts = [jnp.dot(mat[pl.ds(at, edge), :], e, preferred_element_type=F32) for at in (0, edge)]
-        else:
-            rows = pl.ds(2 * edge, cells - 2 * edge)
-            parts = [jnp.dot(mat[rows, :k_half], e[:k_half], preferred_element_type=F32)
-                     + jnp.dot(mat[rows, k_half:], e[k_half:], preferred_element_type=F32)]
-        parts = [z.astype(BF16).astype(F32) for z in parts]
-        if group == 0:
-            return (0, depth, parts[0]), (sub - depth, depth, parts[1])
-        return ((depth, sub - 2 * depth, parts[0]),)
+    def dots(at, count, e, cuts):
+        return sum(jnp.dot(mat[pl.ds(at, count), lo:hi], e[lo:hi], preferred_element_type=F32)
+                   for lo, hi in zip(cuts[:-1], cuts[1:]))
+
+    middle_rows = cells - 2 * edge
+
+    def solve_ends(e):
+        return [dots(at, edge, e, (0, big * big)).astype(BF16) for at in (0, edge)]
 
     def update(i, j, width):
         span = pl.ds(j, width)
@@ -337,17 +364,23 @@
     def sweep(t, carry):
         slot = lax.rem(t, 2)
         e = ext[...].reshape(big * big, rhs)
-        for group in range(2):
-            done = solve(group, e)
-            for lo, count, z in done:
-                z = z.reshape(count, sub, rhs)
-                zf[pl.ds(halo + 1 + lo, count), pl.ds(halo + 8, sub)] = z
-                stage(slot, lo, count, z, lambda i, j: zf[pl.ds(halo + 1 + i, 8), halo + 8 + j, :])
-            send(slot, [lo for lo, _, _ in done])
+        def z_column(i, j):
+            return zf[pl.ds(halo + 1 + i, 8), halo + 8 + j, :]
+
+        def keep(lo, count, z):
+            z = z.astype(F32).reshape(count, sub, rhs)
+            zf[pl.ds(halo + 1 + lo, count), pl.ds(halo + 8, sub)] = z
+            return z
+
+        ends = [dots(at, edge, e, (0, big * big)) for at in (0, edge)]
+        ends = [keep(lo, depth, z.astype(BF16)) for lo, z in zip((0, sub - depth), ends)]
+        stage_ends(slot, *ends, z_column)
+        middle = dots(2 * edge, middle_rows, e, (0, big * big))
+        stage_middle(slot, keep(depth, sub - 2 * depth, middle.astype(BF16)), z_column)
 
         for i in range(sub):
-            cells = pl.ds(i * sub, sub)
-            u[cells] = u[cells] + omega * zf[halo + 1 + i, pl.ds(halo + 8, sub)]
+            span = pl.ds(i * sub, sub)
+            u[span] = u[span] + omega * zf[halo + 1 + i, pl.ds(halo + 8, sub)]
 
         def r_ready(d):
             r_copy(d).wait_send()
@@ -369,17 +402,19 @@
                 at = 0 if d == N else below
                 zf[pl.ds(at, depth), pl.ds(halo + 8, sub)] = h_v[d, slot].astype(F32).reshape(depth, sub, rhs)
             elif d in (W, E):
-                at, edge = (8, 7) if d == W else (right, right + 8)
-                for lo, count in chunks:
-                    zf[pl.ds(halo + 1 + lo, count), pl.ds(at, 8)] = h_h[d - W, slot, pl.ds(strip_row(lo), count)].astype(F32)
-                for k in range(tiles):
-                    zf[pl.ds(halo + 1 + 8 * k, 8), edge, :] = h_h[d - W, slot, col_at + k].astype(F32)
+                at, edge_at = (8, 7) if d == W else (right, right + 8)
+                rows, cols = strip_parts(d - W, slot)
+                for lo, t in rows:
+                    zf[pl.ds(halo + 1 + lo, t.shape[0]), pl.ds(at, 8)] = t
+                for lo, t in cols:
+                    zf[pl.ds(halo + 1 + lo, 8), edge_at, :] = t
             else:
                 dr, dc = DIRS[d]
-                at, edge = (8, 7) if dc < 0 else (right, right + 8)
-                start, edge_start = (0, 1) if dr < 0 else (below, below)
-                zf[pl.ds(start, depth), pl.ds(at, 8)] = h_c[slot, d - NW, pl.ds(0, depth)].astype(F32)
-                zf[pl.ds(edge_start, 8), edge, :] = h_c[slot, d - NW, depth].astype(F32)
+                at, edge_at = (8, 7) if dc < 0 else (right, right + 8)
+                start_at, edge_start = (0, 1) if dr < 0 else (below, below)
+                rows, column = corner_parts(d, slot)
+                zf[pl.ds(start_at, depth), pl.ds(at, 8)] = rows
+                zf[pl.ds(edge_start, 8), edge_at, :] = column
 
         each(put_z, (N, S))
         for i in (*range(halo + 1), *range(halo + sub - 1, big)):
@@ -407,16 +442,10 @@
 
     lax.fori_loop(0, SWEEPS - 1, sweep, 0)
     e = ext[...].reshape(big * big, rhs)
-    for group in range(2):
-        for lo, count, z in solve(group, e):
-            span = pl.ds(lo * sub, count * sub)
-            u[span] = u[span] + omega * z
-
-
-def write_out(u_ref, out_hbm, sem):
-    copy = pltpu.make_async_copy(u_ref, out_hbm, sem)
-    copy.start()
-    copy.wait()
+    near, far = solve_ends(e)
+    z_last[pl.ds(0, edge)] = near
+    z_last[pl.ds(cells - edge, edge)] = far
+    z_last[pl.ds(edge, middle_rows)] = dots(2 * edge, middle_rows, e, (0, 1280, big * big)).astype(BF16)
 
 
 def solution(mesh):
@@ -431,12 +460,14 @@
         halo = (big - sub) // 2
         tiles = sub // 8
         dma, vmem = pltpu.SemaphoreType.DMA, pltpu.VMEM
-        flat = jax.ShapeDtypeStruct((sub * sub, rhs), F32)
-        u_new = pl.pallas_call(
+        first, second = 2 * (halo + 1) + 2, sub - 2 * (halo + 1) + tiles - 2
+        buffers = [vmem((2, 2, halo + 1, tiles, 8, rhs), BF16), vmem((2, 2, 3 * first // 4, 8, 128), BF16),
+                   vmem((2, 2, 3 * second // 4, 8, 128), BF16), vmem((2, 4, 3 * halo // 4 + 2, 8, 128), BF16)]
+        u_new, z_last = pl.pallas_call(
             functools.partial(kernel, (row_count, col_count, sub, halo, rhs)),
-            out_shape=pltpu.VMEM(flat.shape, F32),
+            out_shape=(pltpu.VMEM((sub * sub, rhs), F32), pltpu.VMEM((sub * sub, rhs), BF16)),
             in_specs=[pl.BlockSpec(memory_space=pl.ANY)] * 5,
-            out_specs=pl.BlockSpec(memory_space=pltpu.VMEM),
+            out_specs=[pl.BlockSpec(memory_space=pltpu.VMEM)] * 2,
             scratch_shapes=[
                 vmem((rows, cols), BF16), vmem((big, big, rhs), F32),
                 vmem((big, big, rhs), BF16), vmem((big + 2, big + 16, rhs), F32),
@@ -444,20 +475,14 @@
                 vmem((sub, 128), F32), vmem((sub, sub), F32), vmem((8, sub, 128), F32),
                 vmem((2, sub, rhs), F32), vmem((2, sub, rhs), F32), vmem((2, sub, rhs), F32),
                 pltpu.SMEM((1, 1), F32),
-                vmem((2, 2, halo + 1, tiles, 8, rhs), BF16), vmem((2, 2, sub + tiles, 8, rhs), BF16),
-                vmem((2, 4, halo + 2, 8, rhs), BF16),
-                vmem((2, 2, halo + 1, tiles, 8, rhs), BF16), vmem((2, 2, sub + tiles, 8, rhs), BF16),
-                vmem((2, 4, halo + 2, 8, rhs), BF16),
+                *buffers,
+                *buffers,
                 dma((7,)), dma((4,)), dma((4,)), dma((8,)), dma((8,)), dma((8,)), dma((8,)),
-                dma((2, 4, 8)), dma((2, 4, 8)),
+                dma((2, 2, 8)), dma((2, 2, 8)),
             ],
             compiler_params=pltpu.CompilerParams(collective_id=0, has_side_effects=True),
         )(omega_relax.reshape(1, 1), f_blk, u_blk.reshape(sub * sub, rhs), kappa_blk, mat_blk.reshape(rows, cols))
-        out = pl.pallas_call(
-            write_out, out_shape=flat,
-            in_specs=[pl.BlockSpec(memory_space=pltpu.VMEM)], out_specs=pl.BlockSpec(memory_space=pl.ANY),
-            scratch_shapes=[dma],
-        )(u_new)
+        out = u_new + omega_relax * z_last.astype(F32)
         return out.reshape(sub, sub, rhs)
 
     return jax.shard_map(device_fn, mesh=mesh,

time: 57.6 us -> 52.5 us (0.911)
  Pallas kernels: 55.3 us -> 50.8 us
  other arithmetic: 0 us -> 0.85 us
  local copies, waits for them, and re-layouts: 0.78 us -> 0 us
    pallas_call x1, Pallas kernels: 53.5 us -> 50.8 us  [device_fn(): pl.pallas_call(functools.partial(kernel, (row_count, col_count, sub, halo...]
    pallas_call x1 -> x0, Pallas kernels: 1.84 us -> none  [device_fn(): pl.pallas_call(write_out, out_shape=flat, in_specs=[pl.BlockSpec(memory_s...]
    add x0 -> x1, other arithmetic: none -> 0.85 us  [device_fn(): out = u_new + omega_relax * z_last.astype(F32)]
    unnamed x2 -> x0, local copies, waits for them, and re-layouts: 0.78 us -> none
where the time goes in v3:
time: 52.5 us; the launch traced here: 52.3 us
  Pallas kernels  50.8 us (97%)
  other arithmetic  0.85 us (2%)
  between operations  0.66 us (1%)
    pallas_call x1, Pallas kernels, device_fn(): pl.pallas_call(functools.partial(kernel, (row_count, col_count, sub, halo...  50.8 us

profile of v3, /device:TPU:121, one launch (start us, length us, event | category | flops | bytes accessed | tf_op | source)
XLA Modules:
  0.0 52.3 jit_solution(4137166319095537254)
XLA Ops:
  0.7 50.8 %shard_map.55 = (f32[1024,96]{1,0:T(8,128)S(1)}, bf16[1024,96]{1,0:T(8,128)(2,1)S(1)}) custom-call(f32[1,1]{1,0:T(1,128)} %bitcast.4.w_hbm, f32[32,32,96]{2,1,0:T(8,128)} %f_hbm.1, f32[1024,96]{1,0:T(8,128)} %bitcast.6, f32[32,32]{1,0:T(8,128)} %k_hbm.1, bf16[1024,2304]{1,0:T(8,128)(2,1)} %bitcast.5), custom_call_target="tpu_custom_call" | custom-call | tf_op jit(solution)/shard_map/pallas_call | solution.py:466
  51.4 0.8 %multiply_add_fusion = f32[1024,96]{1,0:T(8,128)} fusion(f32[1024,96]{1,0:T(8,128)S(1)} %get-tuple-element.7, bf16[1024,96]{1,0:T(8,128)(2,1)S(1)} %get-tuple-element.8, f32[]{:T(128)} %copy.6), kind=kLoop, calls=%fused_computation | loop fusion | flops 294912 | bytes 983044 | tf_op jit(solution)/shard_map/add | solution.py:485
